TPU v7x, 128 devices: a whole 4x4x4 slice. The times are simulated.
128 devices in a mesh: ctx: 16 (over z, x), tp: 8 (over y, core).
Axes of the slice: x: 4, y: 4, z: 4, core: 2. Of those that a mesh axis runs over, the one named last changes fastest.
Arguments:
- hidden_in: bfloat16 [8192, 5376], P(('ctx', 'tp')), may hold values from -6 to 6
- stretch_start: int32 [1], replicated, may hold values from 1 to 1024
- pre_gain: float32 [5376], replicated, may hold values from 0.1 to 1.9
- q_weight: bfloat16 [5376, 4096], P('ctx', 'tp'), may hold values from -1 to 1
- k_weight: bfloat16 [5376, 2048], P('ctx', 'tp'), may hold values from -1 to 1
- v_weight: bfloat16 [5376, 2048], P('ctx', 'tp'), may hold values from -0.078125 to 0.078125
- o_weight: bfloat16 [4096, 5376], P('tp', 'ctx'), may hold values from -0.09375 to 0.09375
- q_gain: float32 [128], replicated, may hold values from 0.5 to 5
- k_gain: float32 [128], replicated, may hold values from 0.5 to 5
- prior_keys: bfloat16 [1024, 2048], P(None, 'tp'), may hold values from -6 to 6
- prior_values: bfloat16 [1024, 2048], P(None, 'tp'), may hold values from -6 to 6
- post_gain: float32 [5376], replicated, may hold values from 0.1 to 1.9
Outputs:
- result: bfloat16 [8192, 5376], P(('ctx', 'tp'))
All inputs are finite; a program needn't handle non-finite values.
Results may differ from a plain program's by a relative error of at most 0.013.
Values may be sent and summed in bfloat16 or wider, within the bound.
A program may use at most 128 MiB of HBM per device.

v0:
```python
import jax
import jax.numpy as jnp
from jax import lax
from jax.sharding import PartitionSpec as P

HD = 128
WINDOW = 1024


EPSILON = 1e-06
QUERY_FACTOR = 168.0 ** (-0.5)


def in_one_piece(arrays, axis, dim, along):
    ends, at = ([], 0)
    for a in arrays[:-1]:
        at += a.shape[along]
        ends.append(at)
    both = jnp.concatenate(arrays, axis=along)
    return tuple(jnp.split(lax.all_gather(both, axis, axis=dim, tiled=True), ends, axis=along))


def from_behind(value, axis, steps):
    count = lax.axis_size(axis)
    leading, last = (max(0, -steps), min(count, count - steps))
    return lax.ppermute(value, axis, [(source, source + steps) for source in range(leading, last)])


def rms_scale(inputs, scales):
    mean_sq = jnp.mean(inputs * inputs, axis=-1, keepdims=True)
    return inputs * lax.rsqrt(mean_sq + EPSILON) * scales


def rotate(inputs, positions):
    half_dim = inputs.shape[-1] // 2
    frequency = 10000.0 ** (-jnp.arange(half_dim, dtype=jnp.float32) / half_dim)
    angles = positions.astype(jnp.float32)[:, None] * frequency[None, :]
    cosines = jnp.cos(angles)[:, None, :]
    sines = jnp.sin(angles)[:, None, :]
    front = inputs[..., :half_dim]
    second = inputs[..., half_dim:]
    return jnp.concatenate(
        [front * cosines - second * sines, second * cosines + front * sines], axis=-1
    )


def local(
    hidden_in,
    stretch_start,
    pre_gain,
    q_weight,
    k_weight,
    v_weight,
    o_weight,
    q_gain,
    k_gain,
    prior_keys,
    prior_values,
    post_gain,
):
    residual_in = hidden_in.astype(jnp.float32)
    normed = rms_scale(residual_in, pre_gain).astype(jnp.bfloat16)
    block_rows = lax.all_gather(normed, "tp", axis=0, tiled=True)
    row_count = block_rows.shape[0]
    query_cols = q_weight.shape[1]
    kv_cols = k_weight.shape[1]

    def add_piece(segment):
        return jnp.dot(block_rows, segment, preferred_element_type=jnp.float32)

    segments = in_one_piece((q_weight, k_weight, v_weight), "ctx", 0, 1)
    query_raw, key_raw, value_raw = tuple((add_piece(segment) for segment in segments))
    local_heads = query_cols // HD
    local_kv = kv_cols // HD
    group = local_heads // local_kv
    chain_pos = lax.axis_index("ctx")
    positions = WINDOW + chain_pos * row_count + jnp.arange(row_count, dtype=jnp.int32)
    query = (
        rotate(rms_scale(query_raw.reshape(row_count, local_heads, HD), q_gain), positions)
        * QUERY_FACTOR
    ).astype(jnp.bfloat16)
    key_rows = (
        rotate(rms_scale(key_raw.reshape(row_count, local_kv, HD), k_gain), positions)
        .astype(jnp.bfloat16)
        .reshape(row_count, kv_cols)
    )
    value_rows = value_raw.astype(jnp.bfloat16)
    reach = WINDOW // row_count
    earlier = []
    current = (key_rows, value_rows)
    for hop_index in range(reach):
        current = from_behind((current[0], current[1]), "ctx", 1)
        earlier.append(current)
    key_parts = []
    value_parts = []
    for hop_index in range(reach - 1, -1, -1):
        source = chain_pos - (hop_index + 1)
        offset = jnp.maximum(WINDOW + source * row_count, 0)
        cached_keys = lax.dynamic_slice_in_dim(prior_keys, offset, row_count, 0)
        cached_values = lax.dynamic_slice_in_dim(prior_values, offset, row_count, 0)
        key_parts.append(jnp.where(source < 0, cached_keys, earlier[hop_index][0]))
        value_parts.append(jnp.where(source < 0, cached_values, earlier[hop_index][1]))
    key_parts.append(key_rows)
    value_parts.append(value_rows)
    span = (reach + 1) * row_count
    all_keys = jnp.concatenate(key_parts, axis=0).reshape(span, local_kv, HD)
    all_values = jnp.concatenate(value_parts, axis=0).reshape(span, local_kv, HD)
    key_anchor = WINDOW + (chain_pos - reach) * row_count
    query_grouped = query.reshape(row_count, local_kv, group, HD)
    scores = jnp.einsum(
        "qhgd,khd->hgqk", query_grouped, all_keys, preferred_element_type=jnp.float32
    )
    key_pos = key_anchor + jnp.arange(span, dtype=jnp.int32)
    first_valid = WINDOW - stretch_start[0]
    allowed = (
        (key_pos[None, :] <= positions[:, None])
        & (key_pos[None, :] > positions[:, None] - WINDOW)
        & (key_pos[None, :] >= first_valid)
    )
    scores = jnp.where(allowed[None, None, :, :], scores, jnp.float32(-1e30))
    largest = jnp.max(scores, axis=-1, keepdims=True)
    expon = jnp.exp(scores - largest)
    attn_probs = (expon / jnp.sum(expon, axis=-1, keepdims=True)).astype(jnp.bfloat16)
    attended = jnp.einsum(
        "hgqk,khd->qhgd", attn_probs, all_values, preferred_element_type=jnp.float32
    )
    attended = attended.astype(jnp.bfloat16).reshape(row_count, query_cols)
    partial_rows = jnp.dot(
        attended,
        lax.all_gather(o_weight, "ctx", axis=1, tiled=True),
        preferred_element_type=jnp.float32,
    )
    summed = lax.psum_scatter(
        partial_rows.astype(jnp.bfloat16), "tp", scatter_dimension=0, tiled=True
    ).astype(jnp.float32)
    return (residual_in + rms_scale(summed, post_gain)).astype(jnp.bfloat16)


def solution(mesh):
    return jax.shard_map(
        local,
        mesh=mesh,
        in_specs=(
            P(("ctx", "tp"), None),
            P(),
            P(),
            P("ctx", "tp"),
            P("ctx", "tp"),
            P("ctx", "tp"),
            P("tp", "ctx"),
            P(),
            P(),
            P(None, "tp"),
            P(None, "tp"),
            P(),
        ),
        out_specs=P(("ctx", "tp"), None),
        check_vma=False,
    )
```

profile of v0, /device:TPU:32, one launch (start us, length us, event | category | flops | bytes accessed | tf_op | source)
XLA Modules:
  0.0 255.5 jit_solution(17121036638809811373)
XLA Ops:
  6.5 0.0 all-gather.4.cloned.1.call-start
  6.5 1.3 fusion.15
  7.9 2.2 fusion.17
  10.1 0.0 all-gather.4.cloned.1.call-update
  10.1 0.0 all-gather.6.cloned.1.call-start
  10.1 2.1 pad_maximum_fusion.1
  12.3 0.0 all-gather.6.cloned.1.call-update
  12.3 0.0 all-gather.8.cloned.1.call-start
  12.3 0.7 all-gather.8.cloned.1.call-update
  13.0 0.0 reduce-scatter.2.cloned.1.call-start
  13.8 0.5 multiply_cosine_fusion
  14.3 0.1 copy.25
  14.4 0.1 copy.24
  14.6 1.9 and_and_fusion
  16.5 33.3 %all-gather.4.cloned.1.call-done = bf16[512,5376]{1,0:T(8,128)(2,1)} async-done(((bf16[64,5376]{1,0:T(8,128)(2,1)}), bf16[512,5376]{1,0:T(8,128)(2,1)}) %all-gather.4.cloned.1.call-update) | async-done | bytes 5505040 | tf_op jit(solution)/shard_map/all_gather | solution.py:63
  49.8 84.7 %all-gather.6.cloned.1.call-done = bf16[5376,1024]{1,0:T(8,128)(2,1)} async-done(((bf16[336,1024]{1,0:T(8,128)(2,1)}), bf16[5376,1024]{1,0:T(8,128)(2,1)}) %all-gather.6.cloned.1.call-update) | async-done | bytes 11010064 | tf_op jit(solution)/shard_map/all_gather | solution.py:20
  134.5 5.1 %fusion.20 = bf16[512,256]{1,0:T(8,128)(2,1)S(1)} fusion(bf16[512,5376]{1,0:T(8,128)(2,1)} %all-gather.4.cloned.1.call-done, bf16[5376,1024]{1,0:T(8,128)(2,1)} %all-gather.6.cloned.1.call-done), kind=kOutput, calls=%fused_computation.29 | convolution fusion | flops 1409417216 | bytes 8519680 | tf_op jit(solution)/shard_map/dot_general | solution.py:69
  139.7 0.0 copy-start.3
  139.7 0.0 copy-start.5
  139.7 2.4 collective-permute-start
  142.1 0.0 copy-done.7
  142.1 3.4 %multiply_reduce_fusion.1 = (f32[512,2]{0,1:T(2,128)S(1)}, f32[512,256]{0,1:T(8,128)S(1)}) fusion(bf16[512,5376]{1,0:T(8,128)(2,1)S(1)} %copy-done.7, bf16[5376,1024]{1,0:T(8,128)(2,1)} %all-gather.6.cloned.1.call-done), kind=kOutput, calls=%fused_computation.43 | convolution fusion | flops 1409547264 | bytes 8785920 | tf_op jit(solution)/shard_map/dot_general | solution.py:69
  145.5 0.2 copy.23
  145.7 0.0 copy-done.3
  145.8 0.0 copy-done.5
  145.8 0.2 multiply_multiply_fusion.1
  146.0 0.2 multiply_subtract_fusion.1
  146.2 0.8 copy_bitcast_fusion
  147.1 0.0 copy-start.6
  147.1 3.5 %collective-permute-start.2 = (bf16[512,256]{1,0:T(8,128)(2,1)}, bf16[512,256]{1,0:T(8,128)(2,1)}, u32[]{:S(2)}, u32[]{:S(2)}) collective-permute-start(bf16[512,256]{1,0:T(8,128)(2,1)} %copy_bitcast_fusion), channel_id=1, source_target_pairs={{0,8},{8,16},{16,24},{24,32},{32,40},{40,48},{48,56},{56,64},{64,7... | collective-permute-start | bytes 786440 | tf_op jit(solution)/shard_map/ppermute | solution.py:26
  150.6 6.8 %multiply_reduce_fusion = (f32[512,4]{0,1:T(4,128)S(1)}, f32[512,512]{0,1:T(8,128)S(1)}) fusion(bf16[512,5376]{1,0:T(8,128)(2,1)} %all-gather.4.cloned.1.call-done, bf16[5376,1024]{1,0:T(8,128)(2,1)} %all-gather.6.cloned.1.call-done), kind=kOutput, calls=%fused_computation.33 | convolution fusion | flops 2819094528 | bytes 12066816 | tf_op jit(solution)/shard_map/dot_general | solution.py:69
  157.4 0.0 copy-done.6
  157.4 0.2 multiply_multiply_fusion
  157.6 0.0 collective-permute-done
  157.6 3.1 %collective-permute-start.1 = (bf16[512,256]{1,0:T(8,128)(2,1)}, bf16[512,256]{1,0:T(8,128)(2,1)}, u32[]{:S(2)}, u32[]{:S(2)}) collective-permute-start(bf16[512,256]{1,0:T(8,128)(2,1)} %collective-permute-done), channel_id=1, source_target_pairs={{0,8},{8,16},{16,24},{24,32},{32,40},{40,48},{48,56},{56,64},{64,7... | collective-permute-start | bytes 786440 | tf_op jit(solution)/shard_map/ppermute | solution.py:26
  160.8 0.2 multiply_subtract_fusion
  161.0 0.3 copy.30
  161.3 0.3 copy.29
  161.7 0.0 copy-start.2
  161.7 0.8 maximum_convert_fusion
  162.5 0.4 collective-permute-done.2
  163.0 4.2 %collective-permute-start.3 = (bf16[512,256]{1,0:T(8,128)(2,1)}, bf16[512,256]{1,0:T(8,128)(2,1)}, u32[]{:S(2)}, u32[]{:S(2)}) collective-permute-start(bf16[512,256]{1,0:T(8,128)(2,1)} %collective-permute-done.2), channel_id=1, source_target_pairs={{0,8},{8,16},{16,24},{24,32},{32,40},{40,48},{48,56},{56,64},{64,7... | collective-permute-start | bytes 786440 | tf_op jit(solution)/shard_map/ppermute | solution.py:26
  167.2 2.0 collective-permute-done.1
  169.2 1.4 dynamic-slice_select_fusion.1
  170.6 1.0 pad_maximum_fusion
  171.6 1.2 copy.36
  172.8 5.2 %collective-permute-done.3 = bf16[512,256]{1,0:T(8,128)(2,1)} collective-permute-done((bf16[512,256]{1,0:T(8,128)(2,1)}, bf16[512,256]{1,0:T(8,128)(2,1)}, u32[]{:S(2)}, u32[]{:S(2)}) %collective-permute-start.3) | collective-permute-done | bytes 262176 | tf_op jit(solution)/shard_map/ppermute | solution.py:26
  178.0 0.0 copy-done.2
  178.0 1.2 select_bitcast_fusion.1
  179.2 0.1 copy_bitcast_fusion.1
  179.3 0.0 copy-start.1
  179.4 10.2 %fusion.32 = (f32[2,2,512]{2,1,0:T(2,128)S(1)}, f32[2,2,512,1536]{2,3,1,0:T(8,128)}) fusion(pred[512,1536]{0,1:T(8,128)(4,1)} %and_and_fusion, bf16[512,2,128]{2,0,1:T(8,128)(2,1)} %maximum_convert_fusion, bf16[512,2,128]{2,0,1:T(8,128)(2,1)S(1)} %get-tuple-element.23, bf16[512,2,128]{2,0,1:T(8,128)(2,1)S(1)} %get-tuple-element.24, ...), kind=kOutput, calls=%fused_computation.67 | convolution fusion | flops 817890816 | bytes 15212544 | tf_op jit(solution)/shard_map/sub | solution.py:122
  189.6 0.0 copy-done.1
  189.6 5.7 %fusion.19 = bf16[2,128,2,512]{3,1,2,0:T(8,128)(2,1)S(1)} fusion(bf16[1536,2,128,1]{0,2,3,1:T(8,128)(2,1)S(1)} %bitcast.62, f32[2,2,512,1536]{2,3,1,0:T(8,128)} %get-tuple-element.20, f32[2,2,512]{2,1,0:T(2,128)S(1)} %get-tuple-element.19), kind=kOutput, calls=%fused_computation.28 | convolution fusion | flops 811859968 | bytes 13901824 | tf_op jit(solution)/shard_map/hgqk,khd->qhgd/dot_general | solution.py:124
  195.3 2.5 all-gather.8.cloned.1.call-done
  197.7 7.5 %convolution_convert_fusion = bf16[512,5376]{1,0:T(8,128)(2,1)} fusion(bf16[512,512]{0,1:T(8,128)(2,1)S(1)} %bitcast.64, bf16[512,5376]{0,1:T(8,128)(2,1)} %all-gather.8.cloned.1.call-done), kind=kOutput, calls=%fused_computation.5 | convolution fusion | flops 2821324800 | bytes 11534336 | tf_op jit(solution)/shard_map/dot_general | solution.py:128
  205.2 0.0 copy-start
  205.2 0.0 copy-start.4
  205.2 0.0 reduce-scatter.2.cloned.1.call-update
  205.3 40.1 %reduce-scatter.2.cloned.1.call-done = bf16[64,5376]{1,0:T(8,128)(2,1)} async-done(((bf16[512,5376]{1,0:T(8,128)(2,1)}), bf16[64,5376]{1,0:T(8,128)(2,1)}) %reduce-scatter.2.cloned.1.call-update) | async-done | bytes 688144 | tf_op jit(solution)/shard_map/reduce_scatter | solution.py:133
  245.4 1.3 fusion.13
  246.7 0.0 copy-done
  246.7 0.0 copy-done.4
  246.7 2.3 fusion.18
  (10 shorter events, 0.1 us)
Async XLA Ops:
  6.5 43.3 %all-gather.4.cloned.1.call-start = ((), (), s32[]{:S(2)}) async-start(), calls=%async_computation.1 | async-start | bytes 6193152 | tf_op jit(solution)/shard_map/all_gather | solution.py:63
  10.1 124.4 %all-gather.6.cloned.1.call-start = ((), (), s32[]{:S(2)}) async-start(), calls=%async_computation.2 | async-start | bytes 11698176 | tf_op jit(solution)/shard_map/all_gather | solution.py:20
  12.3 185.5 %all-gather.8.cloned.1.call-start = ((), (), s32[]{:S(2)}) async-start(), calls=%async_computation.3 | async-start | bytes 5849088 | tf_op jit(solution)/shard_map/all_gather | solution.py:130
  13.0 232.4 %reduce-scatter.2.cloned.1.call-start = ((), (), s32[]{:S(2)}) async-start(), calls=%async_computation.4 | async-start | bytes 6193152 | tf_op jit(solution)/shard_map/reduce_scatter | solution.py:133
  134.5 7.5 %copy-start.7 = (bf16[512,5376]{1,0:T(8,128)(2,1)S(1)}, bf16[512,5376]{1,0:T(8,128)(2,1)}, u32[]{:S(2)}) copy-start(bf16[512,5376]{1,0:T(8,128)(2,1)} %all-gather.4.cloned.1.call-done) | copy-start | bytes 16515076
  139.7 6.1 %copy-start.3 = (bf16[512,256]{1,0:T(8,128)(2,1)}, bf16[512,256]{1,0:T(8,128)(2,1)S(1)}, u32[]{:S(2)}) copy-start(bf16[512,256]{1,0:T(8,128)(2,1)S(1)} %fusion.20) | copy-start | bytes 786436
  139.7 6.1 %copy-start.5 = (f32[128]{0:T(128)S(1)}, f32[128]{0:T(128)}, u32[]{:S(2)}) copy-start(f32[128]{0:T(128)} %param.20) | copy-start | bytes 1540
  139.7 17.9 %collective-permute-start = (bf16[512,256]{1,0:T(8,128)(2,1)S(1)}, bf16[512,256]{1,0:T(8,128)(2,1)}, u32[]{:S(2)}, u32[]{:S(2)}) collective-permute-start(bf16[512,256]{1,0:T(8,128)(2,1)S(1)} %fusion.20), channel_id=1, source_target_pairs={{0,8},{8,16},{16,24},{24,32},{32,40},{40,48},{48,56},{56,64},{64,7... | collective-permute-start | bytes 786440 | tf_op jit(solution)/shard_map/ppermute | solution.py:26
  147.1 10.3 %copy-start.6 = (f32[128]{0:T(128)S(1)}, f32[128]{0:T(128)}, u32[]{:S(2)}) copy-start(f32[128]{0:T(128)} %param.19) | copy-start | bytes 1540
  147.1 15.9 %collective-permute-start.2 = (bf16[512,256]{1,0:T(8,128)(2,1)}, bf16[512,256]{1,0:T(8,128)(2,1)}, u32[]{:S(2)}, u32[]{:S(2)}) collective-permute-start(bf16[512,256]{1,0:T(8,128)(2,1)} %copy_bitcast_fusion), channel_id=1, source_target_pairs={{0,8},{8,16},{16,24},{24,32},{32,40},{40,48},{48,56},{56,64},{64,7... | collective-permute-start | bytes 786440 | tf_op jit(solution)/shard_map/ppermute | solution.py:26
  157.6 11.6 %collective-permute-start.1 = (bf16[512,256]{1,0:T(8,128)(2,1)}, bf16[512,256]{1,0:T(8,128)(2,1)}, u32[]{:S(2)}, u32[]{:S(2)}) collective-permute-start(bf16[512,256]{1,0:T(8,128)(2,1)} %collective-permute-done), channel_id=1, source_target_pairs={{0,8},{8,16},{16,24},{24,32},{32,40},{40,48},{48,56},{56,64},{64,7... | collective-permute-start | bytes 786440 | tf_op jit(solution)/shard_map/ppermute | solution.py:26
  161.7 16.3 %copy-start.2 = (bf16[1024,256]{1,0:T(8,128)(2,1)S(1)}, bf16[1024,256]{1,0:T(8,128)(2,1)}, u32[]{:S(2)}) copy-start(bf16[1024,256]{1,0:T(8,128)(2,1)} %param.21) | copy-start | bytes 1572868
  163.0 15.0 %collective-permute-start.3 = (bf16[512,256]{1,0:T(8,128)(2,1)}, bf16[512,256]{1,0:T(8,128)(2,1)}, u32[]{:S(2)}, u32[]{:S(2)}) collective-permute-start(bf16[512,256]{1,0:T(8,128)(2,1)} %collective-permute-done.2), channel_id=1, source_target_pairs={{0,8},{8,16},{16,24},{24,32},{32,40},{40,48},{48,56},{56,64},{64,7... | collective-permute-start | bytes 786440 | tf_op jit(solution)/shard_map/ppermute | solution.py:26
  179.3 10.2 %copy-start.1 = (bf16[1536,256]{0,1:T(8,128)(2,1)S(1)}, bf16[1536,256]{0,1:T(8,128)(2,1)}, u32[]{:S(2)}) copy-start(bf16[1536,256]{0,1:T(8,128)(2,1)} %copy.36) | copy-start | bytes 2359300
  205.2 41.5 %copy-start = (bf16[64,5376]{1,0:T(8,128)(2,1)S(1)}, bf16[64,5376]{1,0:T(8,128)(2,1)}, u32[]{:S(2)}) copy-start(bf16[64,5376]{1,0:T(8,128)(2,1)} %param.12) | copy-start | bytes 2064388
  205.2 41.5 %copy-start.4 = (f32[5376]{0:T(1024)S(1)}, f32[5376]{0:T(1024)}, u32[]{:S(2)}) copy-start(f32[5376]{0:T(1024)} %param.23) | copy-start | bytes 64516
Sparse Core Ops, SparseCore 0:
  10.2 39.5 all-gather.3
  52.0 82.5 all-gather.5
  136.7 61.0 all-gather.7
  205.4 39.9 reduce-scatter.1
where the time goes:
time: 257 us; the launch traced here: 256 us
  waiting for transfers between devices  169 us (66%)
  matrix products  38.8 us (15%)
  other arithmetic  17.9 us (7%)
  between operations  14.1 us (5%)
  starting transfers between devices  13.4 us (5%)
    all_gather x1, waiting for transfers between devices, in_one_piece(): lax.all_gather(both, axis, axis=dim, tiled=True)  84.7 us
    reduce_scatter x1, waiting for transfers between devices, local(): lax.psum_scatter(partial_rows.astype(jnp.bfloat16), 'tp', scatter_dimensi...  40.1 us
    all_gather x1, waiting for transfers between devices, local(): block_rows = lax.all_gather(normed, 'tp', axis=0, tiled=True)  33.3 us
    dot_general x3, matrix products, add_piece(): return jnp.dot(block_rows, segment, preferred_element_type=jnp.float32)  15.4 us
    ppermute x4, starting transfers between devices, from_behind(): lax.ppermute(value, axis, [(source, source + steps) for source in range(l...  13.3 us
    sub x1, matrix products, local(): expon = jnp.exp(scores - largest)  10.2 us
    ppermute x4, waiting for transfers between devices, from_behind(): lax.ppermute(value, axis, [(source, source + steps) for source in range(l...  7.66 us
    dot_general x1, matrix products, local(): jnp.dot(attended, lax.all_gather(o_weight, 'ctx', axis=1, tiled=True), pr...  7.5 us
  transfers between devices with their start and end apart: 8, of which 7 were waited for; matrix products, arithmetic and copies ran while one was open for 17% of the time, Pallas kernels for 0%

commit v1 on v0

v1 whole, which is shorter than its diff:
```python
import jax
import jax.numpy as jnp
from jax import lax
from jax.experimental import pallas as pl
from jax.experimental.pallas import tpu as pltpu
from jax.sharding import PartitionSpec as P

HD = 128
WINDOW = 1024
EPSILON = 1e-06
QUERY_FACTOR = 168.0 ** (-0.5)
MESH = pl.DeviceIdType.MESH

D = 5376
BLK = 336
NC = 512
TOK = 512
SUB = 64
CH = 1344
CHP = 1408
SPLIT = ((0, 192, 96), (192, 144, 80))
KT = 768
BF = jnp.bfloat16
F32 = jnp.float32


def body(
    hid_h, start_s, pre_v, q_h, k_h, v_h, o_h, qg_v, kg_v, pk_h, pv_h, post_v, cos_v, sin_v,
    out_v,
    w0, w1, w2, xs, kv, qb, att, acc, hid, pp, dd, ee, gg, cb, ss,
    lsem, wsend, wrecv, xsend, xrecv, kvsend, kvrecv, rsend, rrecv,
):
    c = lax.axis_index("ctx")
    t = lax.axis_index("tp")
    z, x = c // 4, c % 4
    y, core = t // 2, t % 2
    ws = (w0, w1, w2)

    def nxt(a, d):
        return (a + d + 4) % 4

    yp, ym, yo = nxt(y, 1), nxt(y, -1), nxt(y, 2)
    other = 1 - core
    to_yp = {"ctx": c, "tp": yp * 2 + core}
    to_ym = {"ctx": c, "tp": ym * 2 + core}
    to_pt = {"ctx": c, "tp": y * 2 + other}

    def dev(ci):
        return {"ctx": ci, "tp": t}

    own = pl.ds(pl.multiple_of(c * BLK, 16), BLK)
    loads = [
        pltpu.make_async_copy(k_h, w0.at[own, pl.ds(0, 256)], lsem.at[0]),
        pltpu.make_async_copy(v_h, w0.at[own, pl.ds(256, 256)], lsem.at[1]),
        pltpu.make_async_copy(hid_h, hid, lsem.at[2]),
        pltpu.make_async_copy(q_h, w1.at[own, :], lsem.at[3]),
        pltpu.make_async_copy(o_h, w2.at[own, :], lsem.at[4]),
    ]
    for load in loads:
        load.start()

    def prior(g, half, sem):
        rows = pl.ds(half * 512, 512)
        src = (pk_h, pv_h)[g // 2]
        return pltpu.make_async_copy(
            src.at[rows, pl.ds((g % 2) * HD, HD)], kv.at[g, rows, :], lsem.at[sem]
        )

    @pl.when(c == 0)
    def _():
        for g in range(4):
            prior(g, 0, 5 + g).start()
            prior(g, 1, 9 + g).start()

    @pl.when(c == 1)
    def _():
        for g in range(4):
            pltpu.make_async_copy(
                (pk_h, pv_h)[g // 2].at[pl.ds(512, 512), pl.ds((g % 2) * HD, HD)],
                kv.at[g, pl.ds(0, 512), :],
                lsem.at[5 + g],
            ).start()

    barrier = pltpu.get_barrier_semaphore()
    peers = [to_yp, to_ym, to_pt]
    peers += [dev(z * 4 + nxt(x, 1)), dev(z * 4 + nxt(x, -1))]
    peers += [dev(nxt(z, 1) * 4 + x), dev(nxt(z, -1) * 4 + x)]
    peers += [dev((c + 1) % 16), dev((c + 15) % 16)]
    for peer in peers:
        pl.semaphore_signal(barrier, inc=1, device_id=peer, device_id_type=MESH)
    pl.semaphore_wait(barrier, len(peers))

    def fs(col):
        return (x, z) if col == 0 else (z, x)

    def cid(col, f, s):
        return s * 4 + f if col == 0 else f * 4 + s

    def rows_of(col, f, s, part):
        r0, n, h = SPLIT[col]
        off, num = ((r0, n), (r0, h), (r0 + h, n - h))[part]
        return pl.ds(pl.multiple_of(cid(col, f, s) * BLK + off, 16), num)

    def wcopy(p, col, f, s, part, sem, df, ds):
        f0, s0 = fs(col)
        ref = ws[p].at[rows_of(col, f, s, part), :]
        return pltpu.make_async_remote_copy(
            src_ref=ref, dst_ref=ref, send_sem=wsend.at[p], recv_sem=wrecv.at[p, col * 20 + sem],
            device_id=dev(cid(col, nxt(f0, df), nxt(s0, ds))), device_id_type=MESH,
        )

    def got(p, col, f, s, part, sem):
        wcopy(p, col, f, s, part, sem, 1, 0).wait_recv()

    JF = (0, -1, 1, 2)

    def i0(p):
        for col in range(2):
            f, s = fs(col)
            wcopy(p, col, f, s, 0, 0, 1, 0).start()
            wcopy(p, col, f, s, 0, 1, -1, 0).start()
        for col in range(2):
            f, s = fs(col)
            wcopy(p, col, f, s, 0, 4, 0, 1).start()
            wcopy(p, col, f, s, 0, 5, 0, -1).start()

    def s1(p):
        for col in range(2):
            f, s = fs(col)
            got(p, col, nxt(f, -1), s, 0, 0)
            wcopy(p, col, nxt(f, -1), s, 1, 2, 1, 0).start()
            got(p, col, nxt(f, 1), s, 0, 1)
            wcopy(p, col, nxt(f, 1), s, 2, 3, -1, 0).start()
        for col in range(2):
            f, s = fs(col)
            for j in (1, 2):
                fj = nxt(f, JF[j])
                wcopy(p, col, fj, s, 0, 4 + 2 * j, 0, 1).start()
                wcopy(p, col, fj, s, 0, 5 + 2 * j, 0, -1).start()

    def fwd(p, j):
        for col in range(2):
            f, s = fs(col)
            fj = nxt(f, JF[j])
            got(p, col, fj, nxt(s, -1), 0, 4 + 2 * j)
            wcopy(p, col, fj, nxt(s, -1), 1, 12 + 2 * j, 0, 1).start()
            got(p, col, fj, nxt(s, 1), 0, 5 + 2 * j)
            wcopy(p, col, fj, nxt(s, 1), 2, 13 + 2 * j, 0, -1).start()

    def s3(p):
        for col in range(2):
            f, s = fs(col)
            fo = nxt(f, 2)
            got(p, col, fo, s, 1, 2)
            got(p, col, fo, s, 2, 3)
            wcopy(p, col, fo, s, 0, 10, 0, 1).start()
            wcopy(p, col, fo, s, 0, 11, 0, -1).start()

    def last(p, col, j):
        f, s = fs(col)
        fj = nxt(f, JF[j])
        got(p, col, fj, nxt(s, 2), 1, 12 + 2 * j)
        got(p, col, fj, nxt(s, 2), 2, 13 + 2 * j)

    def s6(p):
        for j in range(4):
            for col in range(2):
                last(p, col, j)

    def drain(p):
        ref = ws[p].at[pl.ds(0, 15 * BLK), :]
        pltpu.make_async_remote_copy(
            src_ref=ref, dst_ref=ref, send_sem=wsend.at[p], recv_sem=wrecv.at[p, 0],
            device_id=to_pt, device_id_type=MESH,
        ).wait_send()

    def xcopy(yy, kk, part, sem, to):
        off, num = ((0, SUB), (0, SUB // 2), (SUB // 2, SUB // 2))[part]
        ref = xs.at[pl.ds(pl.multiple_of((yy * 2 + kk) * SUB + off, 16), num), :]
        return pltpu.make_async_remote_copy(
            src_ref=ref, dst_ref=ref, send_sem=xsend, recv_sem=xrecv.at[sem],
            device_id=to, device_id_type=MESH,
        )

    loads[0].wait()
    loads[1].wait()
    i0(0)

    loads[2].wait()

    def prenorm(i, carry):
        rows = pl.ds(pl.multiple_of(i * 16, 16), 16)
        h = hid[rows, :].astype(F32)
        r = lax.rsqrt(jnp.mean(h * h, axis=-1, keepdims=True) + EPSILON)
        xs[pl.ds(pl.multiple_of(t * SUB + i * 16, 16), 16), :] = (h * r * pre_v[...]).astype(BF)
        return carry

    lax.fori_loop(0, SUB // 16, prenorm, 0)
    xcopy(y, core, 0, 0, to_yp).start()
    xcopy(y, core, 0, 1, to_ym).start()
    xcopy(y, core, 0, 4, to_pt).start()

    s1(0)
    fwd(0, 0)
    s3(0)
    fwd(0, 1)
    fwd(0, 2)
    xcopy(ym, core, 0, 0, to_yp).wait_recv()
    xcopy(ym, core, 1, 2, to_yp).start()
    xcopy(ym, core, 0, 5, to_pt).start()
    xcopy(yp, core, 0, 1, to_ym).wait_recv()
    xcopy(yp, core, 2, 3, to_ym).start()
    xcopy(yp, core, 0, 6, to_pt).start()
    loads[3].wait()
    fwd(0, 3)
    i0(1)
    xcopy(yo, core, 1, 2, to_yp).wait_recv()
    xcopy(yo, core, 2, 3, to_yp).wait_recv()
    xcopy(yo, core, 0, 7, to_pt).start()
    s6(0)
    xcopy(y, other, 0, 4, to_pt).wait_recv()
    xcopy(ym, other, 0, 5, to_pt).wait_recv()
    xcopy(yp, other, 0, 6, to_pt).wait_recv()
    xcopy(yo, other, 0, 7, to_pt).wait_recv()

    def mm(w, c0, cols):
        def step(i, carry):
            ks = pl.ds(pl.multiple_of(i * KT, 128), KT)
            acc[:, c0:c0 + cols] += jnp.dot(
                xs[:, ks], w[ks, c0:c0 + cols], preferred_element_type=F32
            )
            return carry

        acc[:, c0:c0 + cols] = jnp.zeros((TOK, cols), F32)
        lax.fori_loop(0, D // KT, step, 0)

    def headed(c0, gain):
        raw = acc[:, c0:c0 + HD]
        r = lax.rsqrt(jnp.mean(raw * raw, axis=-1, keepdims=True) + EPSILON)
        n = raw * r * gain[...]
        return n * cos_v[...] + pltpu.roll(n, HD // 2, 1) * sin_v[...]

    own_rows = pl.ds(WINDOW, TOK)
    mm(w0, 0, 256)
    s1(1)
    mm(w0, 256, 256)
    for g in range(2):
        kv[g, own_rows, :] = headed(g * HD, kg_v).astype(BF)
        kv[2 + g, own_rows, :] = acc[:, 256 + g * HD:256 + (g + 1) * HD].astype(BF)

    def kvcopy(src, dst, sem):
        return pltpu.make_async_remote_copy(
            src_ref=kv.at[:, pl.ds(src, TOK), :], dst_ref=kv.at[:, pl.ds(dst, TOK), :],
            send_sem=kvsend.at[sem], recv_sem=kvrecv.at[sem],
            device_id=dev((c + 1) % 16), device_id_type=MESH,
        )

    @pl.when(c < 15)
    def _():
        kvcopy(1024, 512, 0).start()

    fwd(1, 0)
    s3(1)
    fwd(1, 1)
    fwd(1, 2)

    @pl.when(c >= 1)
    def _():
        kvcopy(512, 512, 0).wait_recv()

    @pl.when((c >= 1) & (c < 15))
    def _():
        kvcopy(512, 0, 1).start()

    loads[4].wait()
    fwd(1, 3)
    i0(2)
    s6(1)

    mm(w1, 0, 256)
    s1(2)
    mm(w1, 256, 256)
    for h in range(4):
        qb[h, :, :] = (headed(h * HD, qg_v) * QUERY_FACTOR).astype(BF)

    @pl.when(c == 0)
    def _():
        for g in range(4):
            prior(g, 0, 5 + g).wait()
            prior(g, 1, 9 + g).wait()

    @pl.when(c == 1)
    def _():
        for g in range(4):
            pltpu.make_async_copy(
                (pk_h, pv_h)[g // 2].at[pl.ds(512, 512), pl.ds((g % 2) * HD, HD)],
                kv.at[g, pl.ds(0, 512), :],
                lsem.at[5 + g],
            ).wait()

    fwd(2, 0)

    @pl.when(c >= 2)
    def _():
        kvcopy(512, 0, 1).wait_recv()

    first = WINDOW - start_s[0] - c * TOK

    def unit(u, carry):
        g, qc = u // 4, u % 4
        q0 = pl.multiple_of(qc * 128, 128)
        q = qb[pl.ds(2 * g, 2), pl.ds(q0, 128), :].reshape(256, HD)
        k = kv[g, pl.ds(q0, 1152), :]
        v = kv[2 + g, pl.ds(q0, 1152), :]
        s = lax.dot_general(q, k, (((1,), (1,)), ((), ())), preferred_element_type=F32)
        j = lax.broadcasted_iota(jnp.int32, (256, 1152), 1)
        r = lax.broadcasted_iota(jnp.int32, (256, 1152), 0)
        r = jnp.where(r >= 128, r - 128, r)
        s = jnp.where((j > r) & (j <= r + WINDOW) & (j >= first - q0), s, F32(-1e30))
        m = jnp.max(s, axis=-1, keepdims=True)
        e = jnp.exp(s - m)
        total = jnp.sum(e, axis=-1, keepdims=True)
        o = jnp.dot(e.astype(BF), v, preferred_element_type=F32) / total
        c0 = pl.multiple_of(g * 256, 128)
        att[pl.ds(q0, 128), pl.ds(c0, 128)] = o[:128].astype(BF)
        c1 = pl.multiple_of(g * 256 + 128, 128)
        att[pl.ds(q0, 128), pl.ds(c1, 128)] = o[128:].astype(BF)
        return carry

    lax.fori_loop(0, 2, unit, 0)
    s3(2)
    lax.fori_loop(2, 4, unit, 0)
    fwd(2, 1)
    lax.fori_loop(4, 6, unit, 0)
    fwd(2, 2)
    lax.fori_loop(6, 8, unit, 0)

    zk = (z, nxt(z, -1), nxt(z, 1), nxt(z, 2))

    def rcopy(src, dst, q, sem, to):
        return pltpu.make_async_remote_copy(
            src_ref=src, dst_ref=dst, send_sem=rsend.at[q, sem], recv_sem=rrecv.at[q, sem],
            device_id=to, device_id_type=MESH,
        )

    def r0copy(q):
        return rcopy(pp.at[q, :, other], dd.at[q], q, 0, to_pt)

    def r1copy(q, half):
        return rcopy(
            cb.at[q, 0, pl.ds(half * 32, 32)], ee.at[q, half], q, 1 + half, (to_yp, to_ym)[half]
        )

    def r2copy(q, half):
        return rcopy(cb.at[q, 1 + half], gg.at[q, half], q, 3 + half, (to_yp, to_ym)[half])

    def proj(q):
        rows = pl.ds(pl.multiple_of(zk[q] * CH, 16), CH)

        def part(i, carry):
            a = att[pl.ds(pl.multiple_of(i * 256, 256), 256), :]
            o = lax.dot_general(
                a, w2[rows, :], (((1,), (1,)), ((), ())), preferred_element_type=F32
            ).astype(BF)
            for b in range(4):
                pp[q, i * 2 + b // 2, b % 2, :, 0:CH] = o[b * SUB:(b + 1) * SUB]
            return carry

        lax.fori_loop(0, 2, part, 0)
        r0copy(q).start()

    def both(q, yy):
        return pp[q, yy, core].astype(F32) + dd[q, yy].astype(F32)

    def r1(q):
        r0copy(q).wait_recv()
        cb[q, 0] = both(q, yo).astype(BF)
        r1copy(q, 0).start()
        r1copy(q, 1).start()

    def r2(q):
        r1copy(q, 0).wait_recv()
        a = both(q, yp)
        cb[q, 1, 0:32] = (a[0:32] + ee[q, 0].astype(F32)).astype(BF)
        cb[q, 1, 32:64] = a[32:64].astype(BF)
        r2copy(q, 0).start()
        r1copy(q, 1).wait_recv()
        a = both(q, ym)
        cb[q, 2, 0:32] = a[0:32].astype(BF)
        cb[q, 2, 32:64] = (a[32:64] + ee[q, 1].astype(F32)).astype(BF)
        r2copy(q, 1).start()

    def r3(q):
        r2copy(q, 0).wait_recv()
        r2copy(q, 1).wait_recv()
        ss[zk[q]] = both(q, y) + gg[q, 0].astype(F32) + gg[q, 1].astype(F32)

    for q in range(4):
        for b in range(8):
            pp[q, b // 2, b % 2, :, 1280:CHP] = jnp.zeros((SUB, CHP - 1280), BF)

    last(2, 1, 0)
    proj(0)
    fwd(2, 3)
    last(2, 1, 1)
    proj(1)
    r1(0)
    last(2, 1, 2)
    proj(2)
    r1(1)
    r2(0)
    last(2, 1, 3)
    for j in range(4):
        last(2, 0, j)
    proj(3)
    r1(2)
    r2(1)
    r1(3)
    r2(2)
    r3(0)
    r2(3)
    r3(1)
    r3(2)
    r3(3)

    lane = lax.broadcasted_iota(jnp.int32, (16, 128), 1)

    def final(i, carry):
        rows = pl.ds(pl.multiple_of(i * 16, 16), 16)
        pieces = []
        for pair in range(2):
            a = ss[2 * pair, rows, :]
            b = pltpu.roll(ss[2 * pair + 1, rows, :], 64, 1)
            mid = jnp.where(lane < 64, a[:, 1280:], b[:, :128])
            pieces += [a[:, :1280], mid, b[:, 128:]]
        v = jnp.concatenate(pieces, axis=1)
        r = lax.rsqrt(jnp.mean(v * v, axis=-1, keepdims=True) + EPSILON)
        out_v[rows, :] = (hid[rows, :].astype(F32) + v * r * post_v[...]).astype(BF)
        return carry

    lax.fori_loop(0, SUB // 16, final, 0)

    for p in range(3):
        drain(p)
    ref = xs.at[pl.ds(0, 7 * SUB), :]
    pltpu.make_async_remote_copy(
        src_ref=ref, dst_ref=ref, send_sem=xsend, recv_sem=xrecv.at[0],
        device_id=to_pt, device_id_type=MESH,
    ).wait_send()

    @pl.when(c < 15)
    def _():
        kvcopy(1024, 512, 0).wait_send()

    @pl.when((c >= 1) & (c < 15))
    def _():
        kvcopy(512, 0, 1).wait_send()

    for q in range(4):
        r0copy(q).wait_send()
        for half in range(2):
            r1copy(q, half).wait_send()
            r2copy(q, half).wait_send()


def local(
    hidden_in, stretch_start, pre_gain, q_weight, k_weight, v_weight, o_weight, q_gain, k_gain,
    prior_keys, prior_values, post_gain,
):
    c = lax.axis_index("ctx")
    positions = (WINDOW + c * TOK + jnp.arange(TOK, dtype=jnp.int32)).astype(F32)
    frequency = 10000.0 ** (-jnp.arange(HD // 2, dtype=F32) / (HD // 2))
    angles = positions[:, None] * frequency[None, :]
    cosines, sines = jnp.cos(angles), jnp.sin(angles)
    cos2 = jnp.concatenate([cosines, cosines], axis=1)
    sin2 = jnp.concatenate([-sines, sines], axis=1)
    hbm = pl.BlockSpec(memory_space=pl.ANY)
    vm = pl.BlockSpec(memory_space=pltpu.VMEM)
    sm = pl.BlockSpec(memory_space=pltpu.SMEM)
    dma = pltpu.SemaphoreType.DMA
    return pl.pallas_call(
        body,
        out_shape=jax.ShapeDtypeStruct((SUB, D), BF),
        in_specs=[hbm, sm, vm, hbm, hbm, hbm, hbm, vm, vm, hbm, hbm, vm, vm, vm],
        out_specs=vm,
        scratch_shapes=[
            pltpu.VMEM((D, NC), BF), pltpu.VMEM((D, NC), BF), pltpu.VMEM((D, NC), BF),
            pltpu.VMEM((TOK, D), BF),
            pltpu.VMEM((4, WINDOW + TOK, HD), BF),
            pltpu.VMEM((4, TOK, HD), BF),
            pltpu.VMEM((TOK, NC), BF),
            pltpu.VMEM((TOK, NC), F32),
            pltpu.VMEM((SUB, D), BF),
            pltpu.VMEM((4, 4, 2, SUB, CHP), BF),
            pltpu.VMEM((4, 4, SUB, CHP), BF),
            pltpu.VMEM((4, 2, SUB // 2, CHP), BF),
            pltpu.VMEM((4, 2, SUB, CHP), BF),
            pltpu.VMEM((4, 3, SUB, CHP), BF),
            pltpu.VMEM((4, SUB, CHP), F32),
            dma((16,)), dma((3,)), dma((3, 40)), dma, dma((8,)), dma((2,)), dma((2,)),
            dma((4, 5)), dma((4, 5)),
        ],
        compiler_params=pltpu.CompilerParams(
            collective_id=0, has_side_effects=True, vmem_limit_bytes=64 * 1024 * 1024 - 128 * 1024
        ),
        name="layer",
    )(
        hidden_in, stretch_start, pre_gain.reshape(1, D), q_weight, k_weight, v_weight,
        o_weight.T, q_gain.reshape(1, HD), k_gain.reshape(1, HD), prior_keys, prior_values,
        post_gain.reshape(1, D), cos2, sin2,
    )


def solution(mesh):
    return jax.shard_map(
        local,
        mesh=mesh,
        in_specs=(
            P(("ctx", "tp"), None), P(), P(), P("ctx", "tp"), P("ctx", "tp"), P("ctx", "tp"),
            P("tp", "ctx"), P(), P(), P(None, "tp"), P(None, "tp"), P(),
        ),
        out_specs=P(("ctx", "tp"), None),
        check_vma=False,
    )
```

time: 257 us -> 155 us (0.60)
  waiting for transfers between devices: 169 us -> 0 us
  Pallas kernels: 0 us -> 148 us
  matrix products: 38.8 us -> 0 us
  other arithmetic: 17.9 us -> 1.99 us
  between operations: 14.1 us -> 0.69 us
  starting transfers between devices: 13.4 us -> 0 us
    pallas_call x0 -> x1, Pallas kernels: none -> 148 us  [local(): pl.pallas_call(body, out_shape=jax.ShapeDtypeStruct((SUB, D), BF), in_spe...]
    all_gather x3 -> x0, waiting for transfers between devices: 121 us -> none  [the longest x1 84.7 us: in_one_piece(): lax.all_gather(both, axis, axis=dim, tiled=True)]
    reduce_scatter x1 -> x0, waiting for transfers between devices: 40.1 us -> none  [local(): lax.psum_scatter(partial_rows.astype(jnp.bfloat16), 'tp', scatter_dimensi...]
    dot_general x5 -> x0, matrix products: 28.6 us -> none  [the longest x3 15.4 us: add_piece(): return jnp.dot(block_rows, segment, preferred_element_type=jnp.float32)]
    ppermute x4 -> x0, starting transfers between devices: 13.3 us -> none  [from_behind(): lax.ppermute(value, axis, [(source, source + steps) for source in range(l...]
    sub x1 -> x0, matrix products: 10.2 us -> none  [local(): expon = jnp.exp(scores - largest)]
    ppermute x4 -> x0, waiting for transfers between devices: 7.66 us -> none  [from_behind(): lax.ppermute(value, axis, [(source, source + steps) for source in range(l...]
    convert_element_type x5 -> x1, other arithmetic: 6.14 us -> 0.01 us  [local(): (WINDOW + c * TOK + jnp.arange(TOK, dtype=jnp.int32)).astype(F32)]
  transfers between devices with their start and end apart: 8 -> 0, of which waited for: 7 -> 0; matrix products, arithmetic and copies ran while one was open for 17% -> 0% of each run, Pallas kernels for 0% -> 0%
where the time goes in v1:
time: 155 us; the launch traced here: 154 us
  Pallas kernels  148 us (95%)
  local copies, waits for them, and re-layouts  3.98 us (3%)
  other arithmetic  1.99 us (1%)
    pallas_call x1, Pallas kernels, local(): pl.pallas_call(body, out_shape=jax.ShapeDtypeStruct((SUB, D), BF), in_spe...  148 us

profile of v1, /device:TPU:32, one launch (start us, length us, event | category | flops | bytes accessed | tf_op | source)
XLA Modules:
  0.0 154.4 jit_solution(17547854119398278373)
XLA Ops:
  0.7 0.0 copy-start
  0.7 1.4 reshape.23.pre_v
  2.1 0.0 copy-done
  2.1 0.6 reshape.26.post_v
  2.7 1.0 fusion
  3.7 1.0 pad_maximum_fusion
  4.7 147.8 %layer.1 = bf16[64,5376]{1,0:T(8,128)(2,1)} custom-call(bf16[64,5376]{1,0:T(8,128)(2,1)} %hid_h.1, s32[1]{0:T(128)S(6)} %copy.14.start_s, f32[1,5376]{1,0:T(1,128)} %reshape.23.pre_v, bf16[336,512]{1,0:T(8,128)(2,1)} %q_h.1, bf16[336,256]{1,0:T(8,128)(2,1)} %k_h.1, bf16[336,256]{1,0:T(8,128)(2,1)} %v_h.1, bf16[336,512]{1,0:T(8,128)(2,1)} %bitcast.3, ...), custom_call_target="tpu_custom_call" | custom-call | tf_op jit(solution)/shard_map/layer/pallas_call | solution.py:481
  152.4 2.0 %copy.15 = bf16[64,5376]{1,0:T(8,128)(2,1)} copy(bf16[64,5376]{1,0:T(8,128)(2,1)} %layer.1) | data formatting | bytes 1376256
  (2 shorter events, 0.0 us)
Async XLA Ops:
  0.7 1.4 copy-start

commit v2 on v0

v2 whole, which is shorter than its diff:
```python
import jax
import jax.numpy as jnp
from jax import lax
from jax.experimental import pallas as pl
from jax.experimental.pallas import tpu as pltpu
from jax.sharding import PartitionSpec as P

HD = 128
WINDOW = 1024
EPSILON = 1e-06
QUERY_FACTOR = 168.0 ** (-0.5)
MESH = pl.DeviceIdType.MESH

D = 5376
BLK = 336
TOK = 512
PAIR = 1024
SUB = 64
HALF = (0, 336), (0, 176), (176, 160)
ON = (144, 192)
OH = ((0, 144), (0, 80), (80, 64)), ((0, 192), (0, 96), (96, 96))
CW = (576, 768)
CWP = (640, 768)
KT = 768
BF = jnp.bfloat16
F32 = jnp.float32
FL = set()


def body(
    hid_h, start_s, pre_h, q_h, k_h, v_h, o_h, qg_v, kg_v, pk_h, pv_h, post_h, freq_v,
    out_v,
    w0, w1, oa, ob, ow, rb, xs, kv, kr, qb, att, ast, acc, hid, pre, post, cos, sin,
    pp, dd, ee, gg, cb, sa, sb, full,
    lsem, wsend, wrecv, osend, orecv, xsend, xrecv, krsend, krrecv, kfsend, kfrecv,
    swsend, swrecv, rsend, rrecv,
):
    c = lax.axis_index("ctx")
    t = lax.axis_index("tp")
    z, x = c // 4, c % 4
    y, core = t // 2, t % 2
    b = x % 2
    nb = 1 - b
    ws = (w0, w1)

    def nxt(a, d):
        return (a + d + 4) % 4

    def pairx(xx):
        return xx + 1 - 2 * (xx % 2)

    def otherx(xx):
        return (xx + 3 + 2 * (xx % 2)) % 4

    xq, xn, xo = pairx(x), otherx(x), nxt(x, 2)
    yp, ym, yo = nxt(y, 1), nxt(y, -1), nxt(y, 2)
    other = 1 - core
    to_yp = {"ctx": c, "tp": yp * 2 + core}
    to_ym = {"ctx": c, "tp": ym * 2 + core}
    to_pt = {"ctx": c, "tp": y * 2 + other}

    def dev(ci):
        return {"ctx": ci, "tp": t}

    to_xq, to_xn = dev(z * 4 + xq), dev(z * 4 + xn)
    to_zp, to_zm = dev(nxt(z, 1) * 4 + x), dev(nxt(z, -1) * 4 + x)

    def remote(src, dst, ssem, rsem, to):
        return pltpu.make_async_remote_copy(
            src_ref=src, dst_ref=dst, send_sem=ssem, recv_sem=rsem, device_id=to,
            device_id_type=MESH,
        )

    own = pl.ds(pl.multiple_of(c * BLK, 16), BLK)
    hc = pl.ds(pl.multiple_of(b * HD, HD), HD)
    lo, hi = pl.ds(0, HD), pl.ds(HD, HD)
    loads0 = [
        pltpu.make_async_copy(k_h.at[:, lo], ow.at[0, 0, :, lo], lsem.at[0]),
        pltpu.make_async_copy(v_h.at[:, lo], ow.at[0, 0, :, hi], lsem.at[1]),
        pltpu.make_async_copy(k_h.at[:, hi], ow.at[0, 1, :, lo], lsem.at[2]),
        pltpu.make_async_copy(v_h.at[:, hi], ow.at[0, 1, :, hi], lsem.at[3]),
        pltpu.make_async_copy(k_h.at[:, hc], w0.at[own, lo], lsem.at[4]),
        pltpu.make_async_copy(v_h.at[:, hc], w0.at[own, hi], lsem.at[5]),
    ]
    loadx = [
        pltpu.make_async_copy(hid_h, hid, lsem.at[6]),
        pltpu.make_async_copy(pre_h, pre.at[0], lsem.at[7]),
    ]
    loads1 = [
        pltpu.make_async_copy(q_h.at[:, pl.ds(0, 256)], ow.at[1, 0], lsem.at[8]),
        pltpu.make_async_copy(q_h.at[:, pl.ds(256, 256)], ow.at[1, 1], lsem.at[9]),
        pltpu.make_async_copy(
            q_h.at[:, pl.ds(pl.multiple_of(b * 256, 256), 256)], w1.at[own, :], lsem.at[10]
        ),
    ]
    loads2 = [
        pltpu.make_async_copy(
            o_h.at[pl.ds(0, ON[0]), :],
            oa.at[pl.ds(pl.multiple_of(c * ON[0], 16), ON[0]), :], lsem.at[11],
        ),
        pltpu.make_async_copy(
            o_h.at[pl.ds(ON[0], ON[1]), :],
            ob.at[pl.ds(pl.multiple_of((x * 4 + z) * ON[1], 16), ON[1]), :], lsem.at[12],
        ),
        pltpu.make_async_copy(post_h, post.at[0], lsem.at[13]),
    ]
    for load in loads0 + loadx + loads1 + loads2:
        load.start()

    def prior(i):
        return pltpu.make_async_copy(
            (pk_h, pv_h)[i].at[:, hc], kv.at[i, pl.ds(0, WINDOW), :], lsem.at[14 + i]
        )

    @pl.when(c < 2)
    def _():
        prior(0).start()
        prior(1).start()

    cq, cn = z * 4 + xq, z * 4 + xn
    behind = (c + 14) % 16
    zb, xb = behind // 4, behind % 4
    barrier = pltpu.get_barrier_semaphore()
    peers = [to_yp, to_ym, to_pt, to_xq, to_xn, to_zp, to_zm]
    peers += [dev((cq + 2) % 16), dev((cn + 2) % 16)]
    peers += [dev(zb * 4 + pairx(xb)), dev(zb * 4 + otherx(xb))]
    for peer in peers:
        pl.semaphore_signal(barrier, inc=1, device_id=peer, device_id_type=MESH)
    pl.semaphore_wait(barrier, len(peers))

    XJ = (x, xq, xn, xo)

    def wrows(zz, xx, part):
        off, num = HALF[part]
        return pl.ds(pl.multiple_of((zz * 4 + xx) * BLK + off, 16), num)

    def wx(p, src, xx, part, sem, to):
        return remote(
            src, ws[p].at[wrows(z, xx, part), :], wsend.at[p], wrecv.at[p, sem], to
        )

    def wz(p, zz, j, part, sem, to):
        ref = ws[p].at[wrows(zz, XJ[j], part), :]
        return remote(ref, ref, wsend.at[p], wrecv.at[p, sem], to)

    def relay_in(p, side, to):
        off, num = HALF[1 + side]
        return remote(
            ow.at[p, b, pl.ds(off, num), :], rb.at[p, side, pl.ds(0, num), :],
            wsend.at[p], wrecv.at[p, 2 + side], to,
        )

    def wx0(p):
        relay_in(p, 0, to_xq).start()
        relay_in(p, 1, to_xn).start()
        wx(p, ow.at[p, nb], x, 0, 0, to_xq).start()
        wx(p, ow.at[p, nb], x, 0, 1, to_xn).start()

    def wz0(p, j):
        wz(p, z, j, 0, 6 + 2 * j, to_zp).start()
        wz(p, z, j, 0, 7 + 2 * j, to_zm).start()

    def wx1(p):
        relay_in(p, 0, to_xq).wait_recv()
        wx(p, rb.at[p, 0, pl.ds(0, HALF[1][1]), :], xq, 1, 4, to_xn).start()
        relay_in(p, 1, to_xn).wait_recv()
        wx(p, rb.at[p, 1, pl.ds(0, HALF[2][1]), :], xn, 2, 5, to_xq).start()

    def wz1(p):
        wx(p, ow.at[p, nb], xq, 0, 0, to_xq).wait_recv()
        wz0(p, 1)
        wx(p, ow.at[p, nb], xn, 0, 1, to_xn).wait_recv()
        wz0(p, 2)

    def wz2(p):
        wx(p, rb.at[p, 0, pl.ds(0, HALF[1][1]), :], xo, 1, 4, to_xn).wait_recv()
        wx(p, rb.at[p, 1, pl.ds(0, HALF[2][1]), :], xo, 2, 5, to_xq).wait_recv()
        wz0(p, 3)

    def wfwd(p, j):
        wz(p, nxt(z, -1), j, 0, 6 + 2 * j, to_zp).wait_recv()
        wz(p, nxt(z, -1), j, 1, 14 + 2 * j, to_zp).start()
        wz(p, nxt(z, 1), j, 0, 7 + 2 * j, to_zm).wait_recv()
        wz(p, nxt(z, 1), j, 2, 15 + 2 * j, to_zm).start()

    def wlast(p):
        for j in range(4):
            wz(p, nxt(z, 2), j, 1, 14 + 2 * j, to_zp).wait_recv()
            wz(p, nxt(z, 2), j, 2, 15 + 2 * j, to_zm).wait_recv()

    JF = (0, -1, 1, 2)

    def fs(col):
        return (x, z) if col == 0 else (z, x)

    def ctx_of(col, f, s):
        return s * 4 + f if col == 0 else f * 4 + s

    def ocopy(col, f, s, part, sem, df, ds):
        f0, s0 = fs(col)
        off, num = OH[col][part]
        ref = (oa, ob)[col].at[pl.ds(pl.multiple_of((s * 4 + f) * ON[col] + off, 16), num), :]
        to = dev(ctx_of(col, nxt(f0, df), nxt(s0, ds)))
        return remote(ref, ref, osend.at[col], orecv.at[col, sem], to)

    def ogot(col, f, s, part, sem):
        ocopy(col, f, s, part, sem, 1, 0).wait_recv()

    def o0(col):
        f, s = fs(col)
        ocopy(col, f, s, 0, 0, 1, 0).start()
        ocopy(col, f, s, 0, 1, -1, 0).start()

    def o0s(col):
        f, s = fs(col)
        ocopy(col, f, s, 0, 4, 0, 1).start()
        ocopy(col, f, s, 0, 5, 0, -1).start()

    def o1(col):
        f, s = fs(col)
        ogot(col, nxt(f, -1), s, 0, 0)
        ocopy(col, nxt(f, -1), s, 1, 2, 1, 0).start()
        ogot(col, nxt(f, 1), s, 0, 1)
        ocopy(col, nxt(f, 1), s, 2, 3, -1, 0).start()

    def o1s(col):
        f, s = fs(col)
        for j in (1, 2):
            fj = nxt(f, JF[j])
            ocopy(col, fj, s, 0, 4 + 2 * j, 0, 1).start()
            ocopy(col, fj, s, 0, 5 + 2 * j, 0, -1).start()

    def o3(col):
        f, s = fs(col)
        fo = nxt(f, 2)
        ogot(col, fo, s, 1, 2)
        ogot(col, fo, s, 2, 3)
        ocopy(col, fo, s, 0, 10, 0, 1).start()
        ocopy(col, fo, s, 0, 11, 0, -1).start()

    def ofwd(col, j):
        f, s = fs(col)
        fj = nxt(f, JF[j])
        ogot(col, fj, nxt(s, -1), 0, 4 + 2 * j)
        ocopy(col, fj, nxt(s, -1), 1, 12 + 2 * j, 0, 1).start()
        ogot(col, fj, nxt(s, 1), 0, 5 + 2 * j)
        ocopy(col, fj, nxt(s, 1), 2, 13 + 2 * j, 0, -1).start()

    def olast(col):
        f, s = fs(col)
        for j in range(4):
            fj = nxt(f, JF[j])
            ogot(col, fj, nxt(s, 2), 1, 12 + 2 * j)
            ogot(col, fj, nxt(s, 2), 2, 13 + 2 * j)

    def xcopy(cc, yy, kk, part, sem, to):
        off, num = ((0, SUB), (0, SUB // 2), (SUB // 2, SUB // 2))[part]
        ref = xs.at[pl.ds(pl.multiple_of(cc * TOK + (yy * 2 + kk) * SUB + off, 16), num), :]
        return remote(ref, ref, xsend, xrecv.at[sem], to)

    def xhop(cc, s):
        xcopy(cc, ym, core, 0, 1 + s, to_yp).wait_recv()
        xcopy(cc, ym, core, 1, 4 + s, to_yp).start()
        xcopy(cc, yp, core, 0, 2 + s, to_ym).wait_recv()
        xcopy(cc, yp, core, 2, 5 + s, to_ym).start()
        xcopy(cc, ym, core, 0, 13 + s // 2, to_pt).start()
        xcopy(cc, yp, core, 0, 14 + s // 2, to_pt).start()

    def xopp(cc, s):
        xcopy(cc, yo, core, 1, 4 + s, to_yp).wait_recv()
        xcopy(cc, yo, core, 2, 5 + s, to_ym).wait_recv()
        xcopy(cc, yo, core, 0, 15 + s // 2, to_pt).start()

    def xsend0(cc, s):
        xcopy(cc, y, core, 0, 1 + s, to_yp).start()
        xcopy(cc, y, core, 0, 2 + s, to_ym).start()
        xcopy(cc, y, core, 0, 3 + s, to_pt).start()

    def xdone(cc, s):
        xcopy(cc, y, other, 0, 3 + s, to_pt).wait_recv()
        xcopy(cc, ym, other, 0, 13 + s // 2, to_pt).wait_recv()
        xcopy(cc, yp, other, 0, 14 + s // 2, to_pt).wait_recv()
        xcopy(cc, yo, other, 0, 15 + s // 2, to_pt).wait_recv()

    for load in loads0:
        load.wait()
    wx0(0)
    wz0(0, 0)
    for load in loadx:
        load.wait()

    def prenorm(i, carry):
        rows = pl.ds(pl.multiple_of(i * 16, 16), 16)
        h = hid[rows, :].astype(F32)
        r = lax.rsqrt(jnp.mean(h * h, axis=-1, keepdims=True) + EPSILON)
        to = pl.ds(pl.multiple_of(b * TOK + t * SUB + i * 16, 16), 16)
        xs[to, :] = (h * r * pre[...]).astype(BF)
        return carry

    lax.fori_loop(0, SUB // 16, prenorm, 0)
    xcopy(b, y, core, 0, 0, to_xq).start()
    xsend0(b, 0)
    for load in loads1:
        load.wait()
    wx0(1)
    wx1(0)
    wz1(0)
    wz2(0)
    for load in loads2:
        load.wait()
    wfwd(0, 0)
    xcopy(nb, y, core, 0, 0, to_xq).wait_recv()
    xsend0(nb, 6)
    wx1(1)
    wfwd(0, 1)
    wfwd(0, 2)
    wz0(1, 0)

    base = WINDOW + (c - b) * TOK

    def angle(i, carry):
        rows = pl.ds(pl.multiple_of(i * 128, 128), 128)
        pos = lax.broadcasted_iota(jnp.int32, (128, HD), 0) + (base + i * 128)
        a = pos.astype(F32) * freq_v[...]
        lane = lax.broadcasted_iota(jnp.int32, (128, HD), 1)
        cos[rows, :] = jnp.cos(a)
        sn = jnp.sin(a)
        sin[rows, :] = jnp.where(lane < HD // 2, -sn, sn)
        return carry

    lax.fori_loop(0, PAIR // 128, angle, 0)
    xhop(b, 0)
    wfwd(0, 3)
    wz1(1)
    wz2(1)
    o0(0)
    o0s(1)
    wlast(0)
    wfwd(1, 0)
    o1(0)
    wfwd(1, 1)
    wfwd(1, 2)
    xhop(nb, 6)
    wfwd(1, 3)
    o0(1)
    o0s(0)
    o1s(0)
    o3(0)
    xopp(b, 0)
    xdone(b, 0)
    wlast(1)
    o1(1)
    xopp(nb, 6)
    xdone(nb, 6)

    def mm(w):
        def step(i, carry):
            ks = pl.ds(pl.multiple_of(i * KT, 128), KT)
            acc[...] += jnp.dot(xs[:, ks], w[ks, :], preferred_element_type=F32)
            return carry

        acc[...] = jnp.zeros((PAIR, 256), F32)
        lax.fori_loop(0, D // KT, step, 0)

    def headed(rows, c0, gain):
        raw = acc[rows, c0:c0 + HD]
        r = lax.rsqrt(jnp.mean(raw * raw, axis=-1, keepdims=True) + EPSILON)
        n = raw * r * gain[...]
        return n * cos[rows, :] + pltpu.roll(n, HD // 2, 1) * sin[rows, :]

    def keys(i, carry):
        rows = pl.ds(pl.multiple_of(i * 128, 128), 128)
        to = pl.ds(pl.multiple_of(WINDOW + i * 128, 128), 128)
        kv[0, to, :] = headed(rows, 0, kg_v).astype(BF)
        kv[1, to, :] = acc[rows, HD:2 * HD].astype(BF)
        return carry

    def queries(i, carry):
        rows = pl.ds(pl.multiple_of(i * 128, 128), 128)
        for h in range(2):
            qb[h, rows, :] = (headed(rows, h * HD, qg_v) * QUERY_FACTOR).astype(BF)
        return carry

    def kcopy(half, i, to):
        return remote(
            kv.at[i, pl.ds(WINDOW + half * TOK, TOK), :], kr.at[half, i],
            krsend.at[half, i], krrecv.at[half, i], to,
        )

    def kfinal(half, i, to):
        return remote(
            kr.at[half, i], kv.at[i, pl.ds(half * TOK, TOK), :],
            kfsend.at[half, i], kfrecv.at[half, i], to,
        )

    mm(w0)
    for half in range(2):
        lax.fori_loop(4 * half, 4 * half + 4, keys, 0)

        @pl.when(c < 14)
        def _():
            for i in range(2):
                kcopy(half, i, (to_xq, to_xn)[half]).start()

    o1s(1)
    o3(1)
    mm(w1)

    def onward(half):
        src = (cq, cn)[half]

        @pl.when(src < 14)
        def _():
            for i in range(2):
                kcopy(half, i, to_xq).wait_recv()
                kfinal(half, i, dev((src + 2) % 16)).start()

    onward(0)
    onward(1)
    lax.fori_loop(0, 8, queries, 0)
    for col in range(2):
        ofwd(col, 0)

    @pl.when(c < 2)
    def _():
        prior(0).wait()
        prior(1).wait()

    @pl.when(c >= 2)
    def _():
        for half in range(2):
            for i in range(2):
                kfinal(half, i, to_xq).wait_recv()

    first = WINDOW - start_s[0] - (c - b) * TOK

    def attend(q0):
        q = qb[:, pl.ds(q0, 128), :].reshape(256, HD)
        k = kv[0, pl.ds(q0, 1152), :]
        v = kv[1, pl.ds(q0, 1152), :]
        s = lax.dot_general(q, k, (((1,), (1,)), ((), ())), preferred_element_type=F32)
        j = lax.broadcasted_iota(jnp.int32, (256, 1152), 1)
        r = lax.broadcasted_iota(jnp.int32, (256, 1152), 0)
        r = jnp.where(r >= 128, r - 128, r)
        s = jnp.where((j > r) & (j <= r + WINDOW) & (j >= first - q0), s, F32(-1e30))
        m = jnp.max(s, axis=-1, keepdims=True)
        e = jnp.exp(s - m)
        total = jnp.sum(e, axis=-1, keepdims=True)
        return (jnp.dot(e.astype(BF), v, preferred_element_type=F32) / total).astype(BF)

    def swap(i):
        rows = pl.ds(pl.multiple_of(i * 128, 128), 128)
        return remote(ast.at[rows, :], att.at[b, rows, :], swsend.at[i], swrecv.at[i], to_xq)

    def unit_pair(i, carry):
        o = attend(pl.multiple_of(nb * TOK + i * 128, 128))
        rows = pl.ds(pl.multiple_of(i * 128, 128), 128)
        ast[rows, 0:128] = o[:128]
        ast[rows, 128:256] = o[128:]
        swap(i).start()
        return carry

    def unit_own(i, carry):
        o = attend(pl.multiple_of(b * TOK + i * 128, 128))
        rows = pl.ds(pl.multiple_of(i * 128, 128), 128)
        att[b, rows, 0:128] = o[:128]
        att[b, rows, 128:256] = o[128:]
        return carry

    lax.fori_loop(0, 4, unit_pair, 0)
    for col in range(2):
        ofwd(col, 1)
        ofwd(col, 2)
    lax.fori_loop(0, 4, unit_own, 0)
    for i in range(4):
        rows = pl.ds(i * 128, 128)
        remote(ast.at[rows, :], att.at[nb, rows, :], swsend.at[i], swrecv.at[i], to_xq).wait_recv()

    CHUNKS = [(0, 0), (1, 0), (0, 1), (0, 2), (1, 1), (1, 2), (0, 3), (1, 3)]

    def at_s(q):
        col, j = CHUNKS[q]
        return nxt(fs(col)[1], JF[j])

    def wide(q):
        return pl.ds(0, CWP[CHUNKS[q][0]])

    def rcopy(src, dst, q, sem, to):
        return remote(src, dst, rsend.at[q, sem], rrecv.at[q, sem], to)

    def r0copy(q):
        return rcopy(pp.at[q, :, other, :, wide(q)], dd.at[q, :, :, wide(q)], q, 0, to_pt)

    def r1copy(q, half):
        return rcopy(
            cb.at[q, 0, pl.ds(half * 32, 32), wide(q)], ee.at[q, half, :, wide(q)], q, 1 + half,
            (to_yp, to_ym)[half],
        )

    def r2copy(q, half):
        return rcopy(
            cb.at[q, 1 + half, :, wide(q)], gg.at[q, half, :, wide(q)], q, 3 + half,
            (to_yp, to_ym)[half],
        )

    def proj(q):
        col = CHUNKS[q][0]
        n = CW[col]
        wref = (oa, ob)[col]
        rows = pl.ds(pl.multiple_of(at_s(q) * n, 16), n)

        def part(i, carry):
            tok = pl.ds(pl.multiple_of(i * 256, 256), 256)
            o = None
            for h in range(2):
                d = lax.dot_general(
                    att[h, tok, :], wref[rows, h * 256:(h + 1) * 256],
                    (((1,), (1,)), ((), ())), preferred_element_type=F32,
                )
                o = d if o is None else o + d
            o = o.astype(BF)
            for g in range(4):
                pp[q, i * 2 + g // 2, g % 2, :, 0:n] = o[g * SUB:(g + 1) * SUB]
            return carry

        lax.fori_loop(0, 2, part, 0)
        r0copy(q).start()

    def both(q, yy):
        w = CWP[CHUNKS[q][0]]
        return pp[q, yy, core, :, 0:w].astype(F32) + dd[q, yy, :, 0:w].astype(F32)

    def r1(q):
        w = CWP[CHUNKS[q][0]]
        r0copy(q).wait_recv()
        cb[q, 0, :, 0:w] = both(q, yo).astype(BF)
        r1copy(q, 0).start()
        r1copy(q, 1).start()

    def r2(q):
        w = CWP[CHUNKS[q][0]]
        r1copy(q, 0).wait_recv()
        a = both(q, yp)
        cb[q, 1, 0:32, 0:w] = (a[0:32] + ee[q, 0, :, 0:w].astype(F32)).astype(BF)
        cb[q, 1, 32:64, 0:w] = a[32:64].astype(BF)
        r2copy(q, 0).start()
        r1copy(q, 1).wait_recv()
        a = both(q, ym)
        cb[q, 2, 0:32, 0:w] = a[0:32].astype(BF)
        cb[q, 2, 32:64, 0:w] = (a[32:64] + ee[q, 1, :, 0:w].astype(F32)).astype(BF)
        r2copy(q, 1).start()

    def r3(q):
        w = CWP[CHUNKS[q][0]]
        r2copy(q, 0).wait_recv()
        r2copy(q, 1).wait_recv()
        v = both(q, y) + gg[q, 0, :, 0:w].astype(F32) + gg[q, 1, :, 0:w].astype(F32)
        (sa, sb)[CHUNKS[q][0]][at_s(q)] = v

    for q in range(8):
        if CHUNKS[q][0] == 0:
            for g in range(8):
                pp[q, g // 2, g % 2, :, 512:640] = jnp.zeros((SUB, 128), BF)

    proj(0)
    proj(1)
    r1(0)
    r1(1)
    for col in range(2):
        ofwd(col, 3)
    proj(2)
    r2(0)
    proj(3)
    r2(1)
    r1(2)
    r1(3)
    proj(4)
    proj(5)
    r2(2)
    r2(3)
    r1(4)
    r1(5)
    olast(0)
    proj(6)
    r3(0)
    r3(1)
    r2(4)
    r1(6)
    olast(1)
    proj(7)
    r2(5)
    r3(2)
    r1(7)
    r3(3)
    r2(6)
    r3(4)
    r2(7)
    r3(5)
    r3(6)
    r3(7)

    for i in range(16):
        zi, xi = i // 4, i % 4
        full[:, i * BLK:i * BLK + ON[0]] = sa[zi, :, xi * ON[0]:(xi + 1) * ON[0]]
        full[:, i * BLK + ON[0]:(i + 1) * BLK] = sb[xi, :, zi * ON[1]:(zi + 1) * ON[1]]

    def final(i, carry):
        rows = pl.ds(pl.multiple_of(i * 16, 16), 16)
        v = full[rows, :]
        r = lax.rsqrt(jnp.mean(v * v, axis=-1, keepdims=True) + EPSILON)
        out_v[rows, :] = (hid[rows, :].astype(F32) + v * r * post[...]).astype(BF)
        return carry

    lax.fori_loop(0, SUB // 16, final, 0)

    for p in range(2):
        remote(ws[p], ws[p], wsend.at[p], wrecv.at[p, 0], to_pt).wait_send()
    for col in range(2):
        ref = (oa, ob)[col].at[pl.ds(0, 15 * ON[col]), :]
        remote(ref, ref, osend.at[col], orecv.at[col, 0], to_pt).wait_send()
    ref = xs.at[pl.ds(0, 15 * SUB), :]
    remote(ref, ref, xsend, xrecv.at[0], to_pt).wait_send()
    for half in range(2):

        @pl.when(c < 14)
        def _():
            for i in range(2):
                kcopy(half, i, to_xq).wait_send()

        @pl.when((cq, cn)[half] < 14)
        def _():
            for i in range(2):
                kfinal(half, i, to_xq).wait_send()

    for i in range(4):
        swap(i).wait_send()
    for q in range(8):
        r0copy(q).wait_send()
        for half in range(2):
            r1copy(q, half).wait_send()
            r2copy(q, half).wait_send()


def local(
    hidden_in, stretch_start, pre_gain, q_weight, k_weight, v_weight, o_weight, q_gain, k_gain,
    prior_keys, prior_values, post_gain,
):
    frequency = 10000.0 ** (-jnp.arange(HD // 2, dtype=F32) / (HD // 2))
    freq2 = jnp.concatenate([frequency, frequency]).reshape(1, HD)
    hbm = pl.BlockSpec(memory_space=pl.ANY)
    vm = pl.BlockSpec(memory_space=pltpu.VMEM)
    sm = pl.BlockSpec(memory_space=pltpu.SMEM)
    dma = pltpu.SemaphoreType.DMA
    return pl.pallas_call(
        body,
        out_shape=jax.ShapeDtypeStruct((SUB, D), BF),
        in_specs=[hbm, sm, hbm, hbm, hbm, hbm, hbm, vm, vm, hbm, hbm, hbm, vm],
        out_specs=vm,
        scratch_shapes=[
            pltpu.VMEM((D, 256), BF), pltpu.VMEM((D, 256), BF),
            pltpu.VMEM((16 * ON[0], 512), BF), pltpu.VMEM((16 * ON[1], 512), BF),
            pltpu.VMEM((2, 2, BLK, 256), BF), pltpu.VMEM((2, 2, 176, 256), BF),
            pltpu.VMEM((PAIR, D), BF),
            pltpu.VMEM((2, WINDOW + PAIR, HD), BF), pltpu.VMEM((2, 2, TOK, HD), BF),
            pltpu.VMEM((2, PAIR, HD), BF),
            pltpu.VMEM((2, TOK, 256), BF), pltpu.VMEM((TOK, 256), BF),
            pltpu.VMEM((PAIR, 256), F32),
            pltpu.VMEM((SUB, D), BF), pltpu.VMEM((1, D), F32), pltpu.VMEM((1, D), F32),
            pltpu.VMEM((PAIR, HD), F32), pltpu.VMEM((PAIR, HD), F32),
            pltpu.VMEM((8, 4, 2, SUB, 768), BF),
            pltpu.VMEM((8, 4, SUB, 768), BF),
            pltpu.VMEM((8, 2, SUB // 2, 768), BF),
            pltpu.VMEM((8, 2, SUB, 768), BF),
            pltpu.VMEM((8, 3, SUB, 768), BF),
            pltpu.VMEM((4, SUB, CWP[0]), F32), pltpu.VMEM((4, SUB, CWP[1]), F32),
            pltpu.VMEM((SUB, D), F32),
            dma((16,)), dma((2,)), dma((2, 22)), dma((2,)), dma((2, 20)), dma, dma((20,)),
            dma((2, 2)), dma((2, 2)), dma((2, 2)), dma((2, 2)), dma((4,)), dma((4,)),
            dma((8, 5)), dma((8, 5)),
        ],
        compiler_params=pltpu.CompilerParams(
            collective_id=0, has_side_effects=True, vmem_limit_bytes=64 * 1024 * 1024 - 128 * 1024
        ),
        name="layer",
    )(
        hidden_in, stretch_start, pre_gain, q_weight, k_weight, v_weight,
        o_weight.T, q_gain.reshape(1, HD), k_gain.reshape(1, HD), prior_keys, prior_values,
        post_gain, freq2,
    )


def solution(mesh):
    return jax.shard_map(
        local,
        mesh=mesh,
        in_specs=(
            P(("ctx", "tp"), None), P(), P(), P("ctx", "tp"), P("ctx", "tp"), P("ctx", "tp"),
            P("tp", "ctx"), P(), P(), P(None, "tp"), P(None, "tp"), P(),
        ),
        out_specs=P(("ctx", "tp"), None),
        check_vma=False,
    )
```

time: 257 us -> 158 us (0.61)
  waiting for transfers between devices: 169 us -> 0 us
  Pallas kernels: 0 us -> 154 us
  matrix products: 38.8 us -> 0 us
  other arithmetic: 17.9 us -> 0.6 us
  between operations: 14.1 us -> 0.67 us
  starting transfers between devices: 13.4 us -> 0 us
    pallas_call x0 -> x1, Pallas kernels: none -> 154 us  [local(): pl.pallas_call(body, out_shape=jax.ShapeDtypeStruct((SUB, D), BF), in_spe...]
    all_gather x3 -> x0, waiting for transfers between devices: 121 us -> none  [the longest x1 84.7 us: in_one_piece(): lax.all_gather(both, axis, axis=dim, tiled=True)]
    reduce_scatter x1 -> x0, waiting for transfers between devices: 40.1 us -> none  [local(): lax.psum_scatter(partial_rows.astype(jnp.bfloat16), 'tp', scatter_dimensi...]
    dot_general x5 -> x0, matrix products: 28.6 us -> none  [the longest x3 15.4 us: add_piece(): return jnp.dot(block_rows, segment, preferred_element_type=jnp.float32)]
    ppermute x4 -> x0, starting transfers between devices: 13.3 us -> none  [from_behind(): lax.ppermute(value, axis, [(source, source + steps) for source in range(l...]
    sub x1 -> x0, matrix products: 10.2 us -> none  [local(): expon = jnp.exp(scores - largest)]
    ppermute x4 -> x0, waiting for transfers between devices: 7.66 us -> none  [from_behind(): lax.ppermute(value, axis, [(source, source + steps) for source in range(l...]
    convert_element_type x5 -> x0, other arithmetic: 6.14 us -> none  [the longest x1 2.26 us: local(): return (residual_in + rms_scale(summed, post_gain)).astype(jnp.bfloat16)]
  transfers between devices with their start and end apart: 8 -> 0, of which waited for: 7 -> 0; matrix products, arithmetic and copies ran while one was open for 17% -> 0% of each run, Pallas kernels for 0% -> 0%
where the time goes in v2:
time: 158 us
  Pallas kernels  154 us (97%)
  local copies, waits for them, and re-layouts  1.99 us (1%)
    pallas_call x1, Pallas kernels, local(): pl.pallas_call(body, out_shape=jax.ShapeDtypeStruct((SUB, D), BF), in_spe...  154 us

profile of v2, /device:TPU:32, one launch (start us, length us, event | category | flops | bytes accessed | tf_op | source)
XLA Modules:
  0.0 157.7 jit_solution(8579800244884113899)
XLA Ops:
  0.7 0.6 maximum_bitcast_fusion.freq_v
  1.3 154.5 %layer.1 = bf16[64,5376]{1,0:T(8,128)(2,1)} custom-call(bf16[64,5376]{1,0:T(8,128)(2,1)} %hid_h.1, s32[1]{0:T(128)S(6)} %copy.14.start_s, f32[5376]{0:T(1024)} %pre_h.1, bf16[336,512]{1,0:T(8,128)(2,1)} %q_h.1, bf16[336,256]{1,0:T(8,128)(2,1)} %k_h.1, bf16[336,256]{1,0:T(8,128)(2,1)} %v_h.1, bf16[336,512]{1,0:T(8,128)(2,1)} %bitcast.5, f32[1,128]{1,0:T(1,128)} %bitcast.6, ...), custom_call_target="tpu_custom_call" | custom-call | tf_op jit(solution)/shard_map/layer/pallas_call | solution.py:654
  155.8 2.0 %copy.15 = bf16[64,5376]{1,0:T(8,128)(2,1)} copy(bf16[64,5376]{1,0:T(8,128)(2,1)} %layer.1) | data formatting | bytes 1376256
  (1 shorter events, 0.0 us)

commit v3 on v2

v3 whole, which is shorter than its diff:
```python
import jax
import jax.numpy as jnp
from jax import lax
from jax.experimental import pallas as pl
from jax.experimental.pallas import tpu as pltpu
from jax.sharding import PartitionSpec as P

HD = 128
WINDOW = 1024
EPSILON = 1e-06
QUERY_FACTOR = 168.0 ** (-0.5)
MESH = pl.DeviceIdType.MESH

D = 5376
BLK = 336
TOK = 512
PAIR = 1024
SUB = 64
HALF = (0, 336), (0, 176), (176, 160)
ON = (144, 192)
OH = ((0, 144), (0, 80), (80, 64)), ((0, 192), (0, 96), (96, 96))
CW = (576, 768)
CWP = (640, 768)
KT = 768
BF = jnp.bfloat16
F32 = jnp.float32
ORDER = (
    "wr,0", "ww,0", "wz0,0", "pn", "xp,1", "xo,0", "xo,1", "xp,0", "wf,0,1", "wf,0,0", "wr,1", "ww,1", "wfw,0,0,0", "wfw,0,0,1", "wzx,0,2",
    "wzx,0,1", "os,0,0,0", "os,0,0,1", "xf,0,0", "wf,1,1", "ang", "zero", "wzx,1,2", "wfw,0,2,0", "wfw,0,2,1", "xg,1", "wfw,0,1,1",
    "wfw,0,1,0", "xm,0,0", "xf,0,1", "xm,0,1", "xg,0", "wfw,1,2,1", "wfw,1,2,0", "wzo,0", "xf,1,1", "wf,1,0", "wz0,1", "wzx,1,1", "wzo,1",
    "wfw,0,3,1", "xopp,0", "wfw,0,3,0", "xd,0", "os,1,0,0", "os,1,0,1", "wfw,1,0,1", "wfw,1,0,0", "of,0,0,0", "of,0,0,1",
    "wfw,1,1,1", "o0,0,0", "o0,0,1", "xf,1,0", "xm,1,0", "xm,1,1", "wfw,1,1,0", "of,1,0,0", "of,1,0,1", "wfw,1,3,1", "wfw,1,3,0",
    "o1,0,0", "o1,0,1", "os,0,1,0", "os,0,2,0", "os,0,1,1", "os,0,2,1", "wl,0", "mk,0", "o0,1,0", "o0,1,1", "o3,0", "os,0,3,0", "os,0,3,1",
    "xopp,1", "xd,1", "mk,1", "kvf,0,0", "kvf,0,1", "wl,1", "mq,0", "of,0,1,1", "mq,1", "kvf,1,0", "kvf,1,1", "of,0,1,0", "of,0,2,1",
    "of,0,2,0", "o1,1,1", "os,1,2,0", "os,1,2,1", "aw", "au,0", "au,1", "au,2", "au,3", "of,0,3,0", "of,0,3,1", "ao,0", "ao,1", "of,1,2,0",
    "of,1,2,1", "ao,2", "ao,3", "o1,1,0", "os,1,1,0", "os,1,1,1", "sw", "pj,0", "pj,2", "pj,3", "r1,0", "pj,6", "r1,2", "of,1,1,1", "o3,1",
    "os,1,3,0", "os,1,3,1", "pj,1", "r1,3", "r1,6", "r2,0,0", "r2,0,1", "r1,1", "r2,2,0", "r2,2,1", "of,1,1,0", "r2,3,0", "r2,3,1", "r2,6,0",
    "r2,6,1", "r3,0", "of,1,3,0", "pj,4", "r2,1,0", "r2,1,1", "of,1,3,1", "pj,5", "r3,2", "r1,4", "r1,5", "r3,3", "pj,7", "r3,6", "r1,7", "r3,1",
    "r2,4,0", "r2,4,1", "r2,5,0", "r2,5,1", "r2,7,0", "r2,7,1", "r3,4", "r3,5", "r3,7",
)


def body(
    hid_h, start_s, pre_h, q_h, k_h, v_h, o_h, qg_v, kg_v, pk_h, pv_h, post_h, freq_v,
    out_v,
    w0, w1, oa, ob, ow, rb, xs, kv, kr, qb, att, ast, acc, hid, pre, post, cos, sin,
    pp, dd, ee, gg, cb, sa, sb, full,
    lsem, wsend, wrecv, osend, orecv, xsend, xrecv, krsend, krrecv, kfsend, kfrecv,
    swsend, swrecv, rsend, rrecv,
):
    c = lax.axis_index("ctx")
    t = lax.axis_index("tp")
    z, x = c // 4, c % 4
    y, core = t // 2, t % 2
    b = x % 2
    nb = 1 - b
    ws = (w0, w1)

    def nxt(a, d):
        return (a + d + 4) % 4

    def pairx(xx):
        return xx + 1 - 2 * (xx % 2)

    def otherx(xx):
        return (xx + 3 + 2 * (xx % 2)) % 4

    xq, xn, xo = pairx(x), otherx(x), nxt(x, 2)
    yp, ym, yo = nxt(y, 1), nxt(y, -1), nxt(y, 2)
    other = 1 - core
    to_yp = {"ctx": c, "tp": yp * 2 + core}
    to_ym = {"ctx": c, "tp": ym * 2 + core}
    to_pt = {"ctx": c, "tp": y * 2 + other}

    def dev(ci):
        return {"ctx": ci, "tp": t}

    to_xq, to_xn = dev(z * 4 + xq), dev(z * 4 + xn)
    to_zp, to_zm = dev(nxt(z, 1) * 4 + x), dev(nxt(z, -1) * 4 + x)

    def remote(src, dst, ssem, rsem, to):
        return pltpu.make_async_remote_copy(
            src_ref=src, dst_ref=dst, send_sem=ssem, recv_sem=rsem, device_id=to,
            device_id_type=MESH,
        )

    own = pl.ds(pl.multiple_of(c * BLK, 16), BLK)
    hc = pl.ds(pl.multiple_of(b * HD, HD), HD)
    lo, hi = pl.ds(0, HD), pl.ds(HD, HD)
    loads0 = [
        pltpu.make_async_copy(k_h.at[:, lo], ow.at[0, 0, :, lo], lsem.at[0]),
        pltpu.make_async_copy(v_h.at[:, lo], ow.at[0, 0, :, hi], lsem.at[1]),
        pltpu.make_async_copy(k_h.at[:, hi], ow.at[0, 1, :, lo], lsem.at[2]),
        pltpu.make_async_copy(v_h.at[:, hi], ow.at[0, 1, :, hi], lsem.at[3]),
        pltpu.make_async_copy(k_h.at[:, hc], w0.at[own, lo], lsem.at[4]),
        pltpu.make_async_copy(v_h.at[:, hc], w0.at[own, hi], lsem.at[5]),
    ]
    loadx = [
        pltpu.make_async_copy(hid_h, hid, lsem.at[6]),
        pltpu.make_async_copy(pre_h, pre.at[0], lsem.at[7]),
    ]
    loads1 = [
        pltpu.make_async_copy(q_h.at[:, pl.ds(0, 256)], ow.at[1, 0], lsem.at[8]),
        pltpu.make_async_copy(q_h.at[:, pl.ds(256, 256)], ow.at[1, 1], lsem.at[9]),
        pltpu.make_async_copy(
            q_h.at[:, pl.ds(pl.multiple_of(b * 256, 256), 256)], w1.at[own, :], lsem.at[10]
        ),
    ]
    loads2 = [
        pltpu.make_async_copy(
            o_h.at[pl.ds(0, ON[0]), :],
            oa.at[pl.ds(pl.multiple_of(c * ON[0], 16), ON[0]), :], lsem.at[11],
        ),
        pltpu.make_async_copy(
            o_h.at[pl.ds(ON[0], ON[1]), :],
            ob.at[pl.ds(pl.multiple_of((x * 4 + z) * ON[1], 16), ON[1]), :], lsem.at[12],
        ),
        pltpu.make_async_copy(post_h, post.at[0], lsem.at[13]),
    ]
    for load in loads0 + loadx + loads1 + loads2:
        load.start()

    def prior(i):
        return pltpu.make_async_copy(
            (pk_h, pv_h)[i].at[:, hc], kv.at[i, pl.ds(0, WINDOW), :], lsem.at[14 + i]
        )

    @pl.when(c < 2)
    def _():
        prior(0).start()
        prior(1).start()

    cq, cn = z * 4 + xq, z * 4 + xn
    behind = (c + 14) % 16
    zb, xb = behind // 4, behind % 4
    barrier = pltpu.get_barrier_semaphore()
    peers = [to_yp, to_ym, to_pt, to_xq, to_xn, to_zp, to_zm]
    peers += [dev((cq + 2) % 16), dev((cn + 2) % 16)]
    peers += [dev(zb * 4 + pairx(xb)), dev(zb * 4 + otherx(xb))]
    for peer in peers:
        pl.semaphore_signal(barrier, inc=1, device_id=peer, device_id_type=MESH)
    pl.semaphore_wait(barrier, len(peers))

    steps = {}

    def step(fn):
        steps[fn.__name__[1:]] = fn
        return fn

    waited = set()

    def need(name, group):
        if name not in waited:
            waited.add(name)
            for load in group:
                load.wait()

    def need_w(p):
        need(p, (loads0, loads1)[p])

    XJ = (x, xq, xn, xo)
    to_z = (to_zp, to_zm)

    def wrows(zz, xx, part):
        off, num = HALF[part]
        return pl.ds(pl.multiple_of((zz * 4 + xx) * BLK + off, 16), num)

    def wx(p, src, xx, part, sem, to):
        return remote(
            src, ws[p].at[wrows(z, xx, part), :], wsend.at[p], wrecv.at[p, sem], to
        )

    def wz(p, zz, j, part, sem, to):
        ref = ws[p].at[wrows(zz, XJ[j], part), :]
        return remote(ref, ref, wsend.at[p], wrecv.at[p, sem], to)

    def relay_in(p, side):
        off, num = HALF[1 + side]
        return remote(
            ow.at[p, b, pl.ds(off, num), :], rb.at[p, side, pl.ds(0, num), :],
            wsend.at[p], wrecv.at[p, 2 + side], (to_xq, to_xn)[side],
        )

    def relay_out(p, side, xx):
        src = rb.at[p, side, pl.ds(0, HALF[1 + side][1]), :]
        return wx(p, src, xx, 1 + side, 4 + side, (to_xn, to_xq)[side])

    def whole(p, side, xx):
        return wx(p, ow.at[p, nb], xx, 0, side, (to_xq, to_xn)[side])

    def wz_out(p, j):
        for i in range(2):
            wz(p, z, j, 0, 6 + 2 * j + i, to_z[i]).start()

    @step
    def _wr(p):
        need_w(p)
        relay_in(p, 0).start()
        relay_in(p, 1).start()

    @step
    def _ww(p):
        need_w(p)
        whole(p, 0, x).start()
        whole(p, 1, x).start()

    @step
    def _wz0(p):
        need_w(p)
        wz_out(p, 0)

    @step
    def _wf(p, side):
        relay_in(p, side).wait_recv()
        relay_out(p, side, (xq, xn)[side]).start()

    @step
    def _wzx(p, j):
        whole(p, j - 1, XJ[j]).wait_recv()
        wz_out(p, j)

    @step
    def _wzo(p):
        relay_out(p, 0, xo).wait_recv()
        relay_out(p, 1, xo).wait_recv()
        wz_out(p, 3)

    @step
    def _wfw(p, j, i):
        zz = nxt(z, (-1, 1)[i])
        wz(p, zz, j, 0, 6 + 2 * j + i, to_z[i]).wait_recv()
        wz(p, zz, j, 1 + i, 14 + 2 * j + i, to_z[i]).start()

    @step
    def _wl(p):
        for j in range(4):
            for i in range(2):
                wz(p, nxt(z, 2), j, 1 + i, 14 + 2 * j + i, to_z[i]).wait_recv()

    JF = (0, -1, 1, 2)

    def fs(col):
        return (x, z) if col == 0 else (z, x)

    def ctx_of(col, f, s):
        return s * 4 + f if col == 0 else f * 4 + s

    def ocopy(col, fj, sj, part, sem, df, ds):
        f0, s0 = fs(col)
        off, num = OH[col][part]
        f, s = nxt(f0, fj), nxt(s0, sj)
        ref = (oa, ob)[col].at[pl.ds(pl.multiple_of((s * 4 + f) * ON[col] + off, 16), num), :]
        to = dev(ctx_of(col, nxt(f0, df), nxt(s0, ds)))
        return remote(ref, ref, osend.at[col], orecv.at[col, sem], to)

    WAY = (1, -1)

    @step
    def _o0(col, i):
        need(2, loads2)
        ocopy(col, 0, 0, 0, i, WAY[i], 0).start()

    @step
    def _o1(col, i):
        ocopy(col, -WAY[i], 0, 0, i, WAY[i], 0).wait_recv()
        ocopy(col, -WAY[i], 0, 1 + i, 2 + i, WAY[i], 0).start()

    @step
    def _o3(col):
        ocopy(col, 2, 0, 1, 2, 1, 0).wait_recv()
        ocopy(col, 2, 0, 2, 3, 1, 0).wait_recv()

    @step
    def _os(col, j, i):
        need(2, loads2)
        ocopy(col, JF[j], 0, 0, 4 + 2 * j + i, 0, WAY[i]).start()

    @step
    def _of(col, j, i):
        ocopy(col, JF[j], -WAY[i], 0, 4 + 2 * j + i, 0, WAY[i]).wait_recv()
        ocopy(col, JF[j], -WAY[i], 1 + i, 12 + 2 * j + i, 0, WAY[i]).start()

    CC = (b, nb)

    def xcopy(cc, yy, kk, part, sem, to):
        off, num = ((0, SUB), (0, SUB // 2), (SUB // 2, SUB // 2))[part]
        row = CC[cc] * TOK + (yy * 2 + kk) * SUB + off
        ref = xs.at[pl.ds(pl.multiple_of(row, 16), num), :]
        return remote(ref, ref, xsend, xrecv.at[sem], to)

    to_y = (to_yp, to_ym)

    def xsem(cc, k):
        return cc * 11 + k

    @step
    def _pn():
        need("x", loadx)

        def prenorm(i, carry):
            rows = pl.ds(pl.multiple_of(i * 16, 16), 16)
            h = hid[rows, :].astype(F32)
            r = lax.rsqrt(jnp.mean(h * h, axis=-1, keepdims=True) + EPSILON)
            to = pl.ds(pl.multiple_of(b * TOK + t * SUB + i * 16, 16), 16)
            xs[to, :] = (h * r * pre[...]).astype(BF)
            return carry

        lax.fori_loop(0, SUB // 16, prenorm, 0)

    @step
    def _xp(h):
        xcopy(0, y, core, 1 + h, 22 + h, to_xq).start()

    def xout(cc, h):
        for i in range(2):
            xcopy(cc, y, core, 1 + h, xsem(cc, 2 * i + h), to_y[i]).start()
        xcopy(cc, y, core, 1 + h, xsem(cc, 6 + h), to_pt).start()

    @step
    def _xo(h):
        xout(0, h)

    @step
    def _xg(h):
        xcopy(1, y, core, 1 + h, 22 + h, to_xq).wait_recv()
        xout(1, h)

    YB = (ym, yp)

    @step
    def _xf(cc, i):
        xcopy(cc, YB[i], core, 1 + i, xsem(cc, 3 * i), to_y[i]).wait_recv()
        xcopy(cc, YB[i], core, 1 + i, xsem(cc, 4 + i), to_y[i]).start()

    @step
    def _xm(cc, i):
        xcopy(cc, YB[i], core, 2 - i, xsem(cc, 1 + i), to_y[i]).wait_recv()
        xcopy(cc, YB[i], core, 0, xsem(cc, 8 + i), to_pt).start()

    @step
    def _xopp(cc):
        xcopy(cc, yo, core, 1, xsem(cc, 4), to_yp).wait_recv()
        xcopy(cc, yo, core, 2, xsem(cc, 5), to_ym).wait_recv()
        xcopy(cc, yo, core, 0, xsem(cc, 10), to_pt).start()

    @step
    def _xd(cc):
        xcopy(cc, y, other, 1, xsem(cc, 6), to_pt).wait_recv()
        xcopy(cc, y, other, 2, xsem(cc, 7), to_pt).wait_recv()
        xcopy(cc, ym, other, 0, xsem(cc, 8), to_pt).wait_recv()
        xcopy(cc, yp, other, 0, xsem(cc, 9), to_pt).wait_recv()
        xcopy(cc, yo, other, 0, xsem(cc, 10), to_pt).wait_recv()

    base = WINDOW + (c - b) * TOK

    @step
    def _ang():
        def angle(i, carry):
            rows = pl.ds(pl.multiple_of(i * 128, 128), 128)
            pos = lax.broadcasted_iota(jnp.int32, (128, HD), 0) + (base + i * 128)
            a = pos.astype(F32) * freq_v[...]
            lane = lax.broadcasted_iota(jnp.int32, (128, HD), 1)
            cos[rows, :] = jnp.cos(a)
            sn = jnp.sin(a)
            sin[rows, :] = jnp.where(lane < HD // 2, -sn, sn)
            return carry

        lax.fori_loop(0, PAIR // 128, angle, 0)

    def mm(w, cc):
        def part(i, carry):
            ks = pl.ds(pl.multiple_of(i * KT, 128), KT)
            rows = pl.ds(pl.multiple_of(CC[cc] * TOK, TOK), TOK)
            acc[...] += jnp.dot(xs[rows, ks], w[ks, :], preferred_element_type=F32)
            return carry

        acc[...] = jnp.zeros((TOK, 256), F32)
        lax.fori_loop(0, D // KT, part, 0)

    def headed(i, cc, c0, gain):
        raw = acc[pl.ds(pl.multiple_of(i * 128, 128), 128), c0:c0 + HD]
        at = pl.ds(pl.multiple_of(CC[cc] * TOK + i * 128, 128), 128)
        r = lax.rsqrt(jnp.mean(raw * raw, axis=-1, keepdims=True) + EPSILON)
        n = raw * r * gain[...]
        return n * cos[at, :] + pltpu.roll(n, HD // 2, 1) * sin[at, :]

    def kcopy(cc, i):
        rows = pl.ds(pl.multiple_of(WINDOW + CC[cc] * TOK, TOK), TOK)
        return remote(
            kv.at[i, rows, :], kr.at[cc, i], krsend.at[cc, i], krrecv.at[cc, i],
            (to_xq, to_xn)[i],
        )

    def kfinal(cc, i, half, to):
        rows = pl.ds(pl.multiple_of(half * TOK, TOK), TOK)
        return remote(
            kr.at[cc, i], kv.at[i, rows, :], kfsend.at[cc, i], kfrecv.at[cc, i], to
        )

    @step
    def _mk(cc):
        mm(w0, cc)

        def keys(i, carry):
            rows = pl.ds(pl.multiple_of(i * 128, 128), 128)
            to = pl.ds(pl.multiple_of(WINDOW + CC[cc] * TOK + i * 128, 128), 128)
            kv[0, to, :] = headed(i, cc, 0, kg_v).astype(BF)
            kv[1, to, :] = acc[rows, HD:2 * HD].astype(BF)
            return carry

        lax.fori_loop(0, 4, keys, 0)

        @pl.when(c < 14)
        def _():
            kcopy(cc, 0).start()
            kcopy(cc, 1).start()

    @step
    def _kvf(cc, i):
        src = (cq, cn)[i]

        @pl.when(src < 14)
        def _():
            kcopy(cc, i).wait_recv()
            kfinal(cc, i, CC[1 - cc], dev((src + 2) % 16)).start()

    @step
    def _mq(cc):
        mm(w1, cc)

        def queries(i, carry):
            to = pl.ds(pl.multiple_of(CC[cc] * TOK + i * 128, 128), 128)
            for h in range(2):
                qb[h, to, :] = (headed(i, cc, h * HD, qg_v) * QUERY_FACTOR).astype(BF)
            return carry

        lax.fori_loop(0, 4, queries, 0)

    @step
    def _aw():
        @pl.when(c < 2)
        def _():
            prior(0).wait()
            prior(1).wait()

        @pl.when(c >= 2)
        def _():
            for cc in range(2):
                for i in range(2):
                    kfinal(cc, i, CC[cc], to_xq).wait_recv()

    first = WINDOW - start_s[0] - (c - b) * TOK

    def attend(q0):
        q = qb[:, pl.ds(q0, 128), :].reshape(256, HD)
        k = kv[0, pl.ds(q0, 1152), :]
        v = kv[1, pl.ds(q0, 1152), :]
        s = lax.dot_general(q, k, (((1,), (1,)), ((), ())), preferred_element_type=F32)
        j = lax.broadcasted_iota(jnp.int32, (256, 1152), 1)
        r = lax.broadcasted_iota(jnp.int32, (256, 1152), 0)
        r = jnp.where(r >= 128, r - 128, r)
        s = jnp.where((j > r) & (j <= r + WINDOW) & (j >= first - q0), s, F32(-1e30))
        m = jnp.max(s, axis=-1, keepdims=True)
        e = jnp.exp(s - m)
        total = jnp.sum(e, axis=-1, keepdims=True)
        return (jnp.dot(e.astype(BF), v, preferred_element_type=F32) / total).astype(BF)

    def swap(i, from_pair):
        rows = pl.ds(i * 128, 128)
        half = nb if from_pair else b
        return remote(ast.at[rows, :], att.at[half, rows, :], swsend.at[i], swrecv.at[i], to_xq)

    @step
    def _au(i):
        o = attend(pl.multiple_of(nb * TOK + i * 128, 128))
        ast[i * 128:(i + 1) * 128, 0:128] = o[:128]
        ast[i * 128:(i + 1) * 128, 128:256] = o[128:]
        swap(i, False).start()

    @step
    def _ao(i):
        o = attend(pl.multiple_of(b * TOK + i * 128, 128))
        att[b, i * 128:(i + 1) * 128, 0:128] = o[:128]
        att[b, i * 128:(i + 1) * 128, 128:256] = o[128:]

    @step
    def _sw():
        for i in range(4):
            swap(i, True).wait_recv()

    CHUNKS = [(0, 0), (1, 0), (0, 1), (0, 2), (1, 1), (1, 2), (0, 3), (1, 3)]

    def at_s(q):
        col, j = CHUNKS[q]
        return nxt(fs(col)[1], JF[j])

    def wide(q):
        return pl.ds(0, CWP[CHUNKS[q][0]])

    def rcopy(src, dst, q, sem, to):
        return remote(src, dst, rsend.at[q, sem], rrecv.at[q, sem], to)

    def r0copy(q):
        return rcopy(pp.at[q, :, other, :, wide(q)], dd.at[q, :, :, wide(q)], q, 0, to_pt)

    def r1copy(q, half):
        return rcopy(
            cb.at[q, 0, pl.ds(half * 32, 32), wide(q)], ee.at[q, half, :, wide(q)], q, 1 + half,
            to_y[half],
        )

    def r2copy(q, half):
        return rcopy(
            cb.at[q, 1 + half, :, wide(q)], gg.at[q, half, :, wide(q)], q, 3 + half, to_y[half],
        )

    def both(q, yy):
        w = CWP[CHUNKS[q][0]]
        return pp[q, yy, core, :, 0:w].astype(F32) + dd[q, yy, :, 0:w].astype(F32)

    @step
    def _pj(q):
        col, j = CHUNKS[q]
        if j == 3:
            for k in range(4):
                for i in range(2):
                    ocopy(col, JF[k], 2, 1 + i, 12 + 2 * k + i, 0, 1).wait_recv()
        n = CW[col]
        wref = (oa, ob)[col]
        rows = pl.ds(pl.multiple_of(at_s(q) * n, 16), n)

        def part(i, carry):
            tok = pl.ds(pl.multiple_of(i * 256, 256), 256)
            o = None
            for h in range(2):
                d = lax.dot_general(
                    att[h, tok, :], wref[rows, h * 256:(h + 1) * 256],
                    (((1,), (1,)), ((), ())), preferred_element_type=F32,
                )
                o = d if o is None else o + d
            o = o.astype(BF)
            for g in range(4):
                pp[q, i * 2 + g // 2, g % 2, :, 0:n] = o[g * SUB:(g + 1) * SUB]
            return carry

        lax.fori_loop(0, 2, part, 0)
        r0copy(q).start()

    @step
    def _r1(q):
        w = CWP[CHUNKS[q][0]]
        r0copy(q).wait_recv()
        cb[q, 0, :, 0:w] = both(q, yo).astype(BF)
        r1copy(q, 0).start()
        r1copy(q, 1).start()

    @step
    def _r2(q, i):
        w = CWP[CHUNKS[q][0]]
        r1copy(q, i).wait_recv()
        a = both(q, (yp, ym)[i])
        add = slice(32 * i, 32 * i + 32)
        rest = slice(32 - 32 * i, 64 - 32 * i)
        cb[q, 1 + i, add, 0:w] = (a[add] + ee[q, i, :, 0:w].astype(F32)).astype(BF)
        cb[q, 1 + i, rest, 0:w] = a[rest].astype(BF)
        r2copy(q, i).start()

    @step
    def _r3(q):
        w = CWP[CHUNKS[q][0]]
        r2copy(q, 0).wait_recv()
        r2copy(q, 1).wait_recv()
        v = both(q, y) + gg[q, 0, :, 0:w].astype(F32) + gg[q, 1, :, 0:w].astype(F32)
        (sa, sb)[CHUNKS[q][0]][at_s(q)] = v

    @step
    def _zero():
        for q in range(8):
            if CHUNKS[q][0] == 0:
                for g in range(8):
                    pp[q, g // 2, g % 2, :, 512:640] = jnp.zeros((SUB, 128), BF)

    for line in ORDER:
        name, *nums = line.split(",")
        steps[name](*[int(v) for v in nums])

    for i in range(16):
        zi, xi = i // 4, i % 4
        full[:, i * BLK:i * BLK + ON[0]] = sa[zi, :, xi * ON[0]:(xi + 1) * ON[0]]
        full[:, i * BLK + ON[0]:(i + 1) * BLK] = sb[xi, :, zi * ON[1]:(zi + 1) * ON[1]]

    def final(i, carry):
        rows = pl.ds(pl.multiple_of(i * 16, 16), 16)
        v = full[rows, :]
        r = lax.rsqrt(jnp.mean(v * v, axis=-1, keepdims=True) + EPSILON)
        out_v[rows, :] = (hid[rows, :].astype(F32) + v * r * post[...]).astype(BF)
        return carry

    lax.fori_loop(0, SUB // 16, final, 0)

    for p in range(2):
        remote(ws[p], ws[p], wsend.at[p], wrecv.at[p, 0], to_pt).wait_send()
    for col in range(2):
        ref = (oa, ob)[col].at[pl.ds(0, 15 * ON[col]), :]
        remote(ref, ref, osend.at[col], orecv.at[col, 0], to_pt).wait_send()
    ref = xs.at[pl.ds(0, 15 * SUB), :]
    remote(ref, ref, xsend, xrecv.at[0], to_pt).wait_send()
    for half in range(2):

        @pl.when(c < 14)
        def _():
            for i in range(2):
                kcopy(half, i).wait_send()

        for i in range(2):

            @pl.when((cq, cn)[i] < 14)
            def _():
                kfinal(half, i, b, to_xq).wait_send()

    for i in range(4):
        swap(i, False).wait_send()
    for q in range(8):
        r0copy(q).wait_send()
        for half in range(2):
            r1copy(q, half).wait_send()
            r2copy(q, half).wait_send()


def local(
    hidden_in, stretch_start, pre_gain, q_weight, k_weight, v_weight, o_weight, q_gain, k_gain,
    prior_keys, prior_values, post_gain,
):
    frequency = 10000.0 ** (-jnp.arange(HD // 2, dtype=F32) / (HD // 2))
    freq2 = jnp.concatenate([frequency, frequency]).reshape(1, HD)
    hbm = pl.BlockSpec(memory_space=pl.ANY)
    vm = pl.BlockSpec(memory_space=pltpu.VMEM)
    sm = pl.BlockSpec(memory_space=pltpu.SMEM)
    dma = pltpu.SemaphoreType.DMA
    return pl.pallas_call(
        body,
        out_shape=jax.ShapeDtypeStruct((SUB, D), BF),
        in_specs=[hbm, sm, hbm, hbm, hbm, hbm, hbm, vm, vm, hbm, hbm, hbm, vm],
        out_specs=vm,
        scratch_shapes=[
            pltpu.VMEM((D, 256), BF), pltpu.VMEM((D, 256), BF),
            pltpu.VMEM((16 * ON[0], 512), BF), pltpu.VMEM((16 * ON[1], 512), BF),
            pltpu.VMEM((2, 2, BLK, 256), BF), pltpu.VMEM((2, 2, 176, 256), BF),
            pltpu.VMEM((PAIR, D), BF),
            pltpu.VMEM((2, WINDOW + PAIR, HD), BF), pltpu.VMEM((2, 2, TOK, HD), BF),
            pltpu.VMEM((2, PAIR, HD), BF),
            pltpu.VMEM((2, TOK, 256), BF), pltpu.VMEM((TOK, 256), BF),
            pltpu.VMEM((TOK, 256), F32),
            pltpu.VMEM((SUB, D), BF), pltpu.VMEM((1, D), F32), pltpu.VMEM((1, D), F32),
            pltpu.VMEM((PAIR, HD), F32), pltpu.VMEM((PAIR, HD), F32),
            pltpu.VMEM((8, 4, 2, SUB, 768), BF),
            pltpu.VMEM((8, 4, SUB, 768), BF),
            pltpu.VMEM((8, 2, SUB // 2, 768), BF),
            pltpu.VMEM((8, 2, SUB, 768), BF),
            pltpu.VMEM((8, 3, SUB, 768), BF),
            pltpu.VMEM((4, SUB, CWP[0]), F32), pltpu.VMEM((4, SUB, CWP[1]), F32),
            pltpu.VMEM((SUB, D), F32),
            dma((16,)), dma((2,)), dma((2, 22)), dma((2,)), dma((2, 20)), dma, dma((24,)),
            dma((2, 2)), dma((2, 2)), dma((2, 2)), dma((2, 2)), dma((4,)), dma((4,)),
            dma((8, 5)), dma((8, 5)),
        ],
        compiler_params=pltpu.CompilerParams(
            collective_id=0, has_side_effects=True, vmem_limit_bytes=64 * 1024 * 1024 - 128 * 1024
        ),
        name="layer",
    )(
        hidden_in, stretch_start, pre_gain, q_weight, k_weight, v_weight,
        o_weight.T, q_gain.reshape(1, HD), k_gain.reshape(1, HD), prior_keys, prior_values,
        post_gain, freq2,
    )


def solution(mesh):
    return jax.shard_map(
        local,
        mesh=mesh,
        in_specs=(
            P(("ctx", "tp"), None), P(), P(), P("ctx", "tp"), P("ctx", "tp"), P("ctx", "tp"),
            P("tp", "ctx"), P(), P(), P(None, "tp"), P(None, "tp"), P(),
        ),
        out_specs=P(("ctx", "tp"), None),
        check_vma=False,
    )
```

time: 158 us -> 126 us (0.80)
  Pallas kernels: 154 us -> 123 us
    pallas_call x1, Pallas kernels: 154 us -> 123 us  [local(): pl.pallas_call(body, out_shape=jax.ShapeDtypeStruct((SUB, D), BF), in_spe...]
where the time goes in v3:
time: 126 us
  Pallas kernels  123 us (98%)
  local copies, waits for them, and re-layouts  1.99 us (2%)
    pallas_call x1, Pallas kernels, local(): pl.pallas_call(body, out_shape=jax.ShapeDtypeStruct((SUB, D), BF), in_spe...  123 us

profile of v3, /device:TPU:32, one launch (start us, length us, event | category | flops | bytes accessed | tf_op | source)
XLA Modules:
  0.0 126.3 jit_solution(11858653312690038702)
XLA Ops:
  0.7 0.6 maximum_bitcast_fusion.freq_v
  1.3 123.1 %layer.1 = bf16[64,5376]{1,0:T(8,128)(2,1)} custom-call(bf16[64,5376]{1,0:T(8,128)(2,1)} %hid_h.1, s32[1]{0:T(128)S(6)} %copy.14.start_s, f32[5376]{0:T(1024)} %pre_h.1, bf16[336,512]{1,0:T(8,128)(2,1)} %q_h.1, bf16[336,256]{1,0:T(8,128)(2,1)} %k_h.1, bf16[336,256]{1,0:T(8,128)(2,1)} %v_h.1, bf16[336,512]{1,0:T(8,128)(2,1)} %bitcast.5, f32[1,128]{1,0:T(1,128)} %bitcast.6, ...), custom_call_target="tpu_custom_call" | custom-call | tf_op jit(solution)/shard_map/layer/pallas_call | solution.py:640
  124.3 2.0 %copy.15 = bf16[64,5376]{1,0:T(8,128)(2,1)} copy(bf16[64,5376]{1,0:T(8,128)(2,1)} %layer.1) | data formatting | bytes 1376256
  (1 shorter events, 0.0 us)

commit v4 on v3

--- a/solution.py
+++ b/solution.py
@@ -17,33 +17,21 @@
 PAIR = 1024
 SUB = 64
 HALF = (0, 336), (0, 176), (176, 160)
-ON = (144, 192)
-OH = ((0, 144), (0, 80), (80, 64)), ((0, 192), (0, 96), (96, 96))
-CW = (576, 768)
-CWP = (640, 768)
-KT = 768
+ON = (192, 144)
+OX = ((0, 0), (0, 192)), ((0, 0), (0, 144))
+OZ = ((0, 96), (96, 96)), ((0, 80), (80, 64))
+CW = (768, 576)
+CWP = (768, 640)
+KT = 2688
+QT = 2688
 BF = jnp.bfloat16
 F32 = jnp.float32
-ORDER = (
-    "wr,0", "ww,0", "wz0,0", "pn", "xp,1", "xo,0", "xo,1", "xp,0", "wf,0,1", "wf,0,0", "wr,1", "ww,1", "wfw,0,0,0", "wfw,0,0,1", "wzx,0,2",
-    "wzx,0,1", "os,0,0,0", "os,0,0,1", "xf,0,0", "wf,1,1", "ang", "zero", "wzx,1,2", "wfw,0,2,0", "wfw,0,2,1", "xg,1", "wfw,0,1,1",
-    "wfw,0,1,0", "xm,0,0", "xf,0,1", "xm,0,1", "xg,0", "wfw,1,2,1", "wfw,1,2,0", "wzo,0", "xf,1,1", "wf,1,0", "wz0,1", "wzx,1,1", "wzo,1",
-    "wfw,0,3,1", "xopp,0", "wfw,0,3,0", "xd,0", "os,1,0,0", "os,1,0,1", "wfw,1,0,1", "wfw,1,0,0", "of,0,0,0", "of,0,0,1",
-    "wfw,1,1,1", "o0,0,0", "o0,0,1", "xf,1,0", "xm,1,0", "xm,1,1", "wfw,1,1,0", "of,1,0,0", "of,1,0,1", "wfw,1,3,1", "wfw,1,3,0",
-    "o1,0,0", "o1,0,1", "os,0,1,0", "os,0,2,0", "os,0,1,1", "os,0,2,1", "wl,0", "mk,0", "o0,1,0", "o0,1,1", "o3,0", "os,0,3,0", "os,0,3,1",
-    "xopp,1", "xd,1", "mk,1", "kvf,0,0", "kvf,0,1", "wl,1", "mq,0", "of,0,1,1", "mq,1", "kvf,1,0", "kvf,1,1", "of,0,1,0", "of,0,2,1",
-    "of,0,2,0", "o1,1,1", "os,1,2,0", "os,1,2,1", "aw", "au,0", "au,1", "au,2", "au,3", "of,0,3,0", "of,0,3,1", "ao,0", "ao,1", "of,1,2,0",
-    "of,1,2,1", "ao,2", "ao,3", "o1,1,0", "os,1,1,0", "os,1,1,1", "sw", "pj,0", "pj,2", "pj,3", "r1,0", "pj,6", "r1,2", "of,1,1,1", "o3,1",
-    "os,1,3,0", "os,1,3,1", "pj,1", "r1,3", "r1,6", "r2,0,0", "r2,0,1", "r1,1", "r2,2,0", "r2,2,1", "of,1,1,0", "r2,3,0", "r2,3,1", "r2,6,0",
-    "r2,6,1", "r3,0", "of,1,3,0", "pj,4", "r2,1,0", "r2,1,1", "of,1,3,1", "pj,5", "r3,2", "r1,4", "r1,5", "r3,3", "pj,7", "r3,6", "r1,7", "r3,1",
-    "r2,4,0", "r2,4,1", "r2,5,0", "r2,5,1", "r2,7,0", "r2,7,1", "r3,4", "r3,5", "r3,7",
-)
 
 
 def body(
     hid_h, start_s, pre_h, q_h, k_h, v_h, o_h, qg_v, kg_v, pk_h, pv_h, post_h, freq_v,
     out_v,
-    w0, w1, oa, ob, ow, rb, xs, kv, kr, qb, att, ast, acc, hid, pre, post, cos, sin,
+    w0, w1, oa, ob, ow, rb, xs, kv, kr, qb, att, ast, acc, accq, hid, pre, post, cos, sin,
     pp, dd, ee, gg, cb, sa, sb, full,
     lsem, wsend, wrecv, osend, orecv, xsend, xrecv, krsend, krrecv, kfsend, kfrecv,
     swsend, swrecv, rsend, rrecv,
@@ -83,6 +71,16 @@
             src_ref=src, dst_ref=dst, send_sem=ssem, recv_sem=rsem, device_id=to,
             device_id_type=MESH,
         )
+
+    cq, cn = z * 4 + xq, z * 4 + xn
+    behind = (c + 14) % 16
+    zb, xb = behind // 4, behind % 4
+    barrier = pltpu.get_barrier_semaphore()
+    peers = [to_yp, to_ym, to_pt, to_xq, to_xn, to_zp, to_zm]
+    peers += [dev((cq + 2) % 16), dev((cn + 2) % 16)]
+    peers += [dev(zb * 4 + pairx(xb)), dev(zb * 4 + otherx(xb))]
+    for peer in peers:
+        pl.semaphore_signal(barrier, inc=1, device_id=peer, device_id_type=MESH)
 
     own = pl.ds(pl.multiple_of(c * BLK, 16), BLK)
     hc = pl.ds(pl.multiple_of(b * HD, HD), HD)
@@ -117,7 +115,7 @@
         ),
         pltpu.make_async_copy(post_h, post.at[0], lsem.at[13]),
     ]
-    for load in loads0 + loadx + loads1 + loads2:
+    for load in loadx + loads0 + loads1 + loads2:
         load.start()
 
     def prior(i):
@@ -130,22 +128,19 @@
         prior(0).start()
         prior(1).start()
 
-    cq, cn = z * 4 + xq, z * 4 + xn
-    behind = (c + 14) % 16
-    zb, xb = behind // 4, behind % 4
-    barrier = pltpu.get_barrier_semaphore()
-    peers = [to_yp, to_ym, to_pt, to_xq, to_xn, to_zp, to_zm]
-    peers += [dev((cq + 2) % 16), dev((cn + 2) % 16)]
-    peers += [dev(zb * 4 + pairx(xb)), dev(zb * 4 + otherx(xb))]
-    for peer in peers:
-        pl.semaphore_signal(barrier, inc=1, device_id=peer, device_id_type=MESH)
+    for load in loadx:
+        load.wait()
+
+    def prenorm(i, carry):
+        rows = pl.ds(pl.multiple_of(i * 16, 16), 16)
+        h = hid[rows, :].astype(F32)
+        r = lax.rsqrt(jnp.mean(h * h, axis=-1, keepdims=True) + EPSILON)
+        to = pl.ds(pl.multiple_of(b * TOK + t * SUB + i * 16, 16), 16)
+        xs[to, :] = (h * r * pre[...]).astype(BF)
+        return carry
+
+    lax.fori_loop(0, SUB // 16, prenorm, 0)
     pl.semaphore_wait(barrier, len(peers))
-
-    steps = {}
-
-    def step(fn):
-        steps[fn.__name__[1:]] = fn
-        return fn
 
     waited = set()
 
@@ -192,93 +187,100 @@
         for i in range(2):
             wz(p, z, j, 0, 6 + 2 * j + i, to_z[i]).start()
 
-    @step
     def _wr(p):
         need_w(p)
         relay_in(p, 0).start()
         relay_in(p, 1).start()
 
-    @step
     def _ww(p):
         need_w(p)
         whole(p, 0, x).start()
         whole(p, 1, x).start()
 
-    @step
     def _wz0(p):
         need_w(p)
         wz_out(p, 0)
 
-    @step
     def _wf(p, side):
         relay_in(p, side).wait_recv()
         relay_out(p, side, (xq, xn)[side]).start()
 
-    @step
     def _wzx(p, j):
         whole(p, j - 1, XJ[j]).wait_recv()
         wz_out(p, j)
 
-    @step
     def _wzo(p):
         relay_out(p, 0, xo).wait_recv()
         relay_out(p, 1, xo).wait_recv()
         wz_out(p, 3)
 
-    @step
     def _wfw(p, j, i):
         zz = nxt(z, (-1, 1)[i])
         wz(p, zz, j, 0, 6 + 2 * j + i, to_z[i]).wait_recv()
         wz(p, zz, j, 1 + i, 14 + 2 * j + i, to_z[i]).start()
 
-    @step
     def _wl(p):
         for j in range(4):
             for i in range(2):
                 wz(p, nxt(z, 2), j, 1 + i, 14 + 2 * j + i, to_z[i]).wait_recv()
 
-    JF = (0, -1, 1, 2)
-
-    def fs(col):
-        return (x, z) if col == 0 else (z, x)
-
-    def ctx_of(col, f, s):
-        return s * 4 + f if col == 0 else f * 4 + s
-
-    def ocopy(col, fj, sj, part, sem, df, ds):
-        f0, s0 = fs(col)
-        off, num = OH[col][part]
-        f, s = nxt(f0, fj), nxt(s0, sj)
-        ref = (oa, ob)[col].at[pl.ds(pl.multiple_of((s * 4 + f) * ON[col] + off, 16), num), :]
-        to = dev(ctx_of(col, nxt(f0, df), nxt(s0, ds)))
+    AX = ((xq, xn), (xq, xn), (1, 0), xo, OX)
+    AZ = ((nxt(z, 1), nxt(z, -1)), (nxt(z, -1), nxt(z, 1)), (0, 1), nxt(z, 2), OZ)
+    AXES = ((AX, AZ), (AZ, AX))
+    HERE = ((x, z), (z, x))
+
+    def first_of(col, j):
+        axis = AXES[col][0]
+        return (HERE[col][0], axis[1][0], axis[1][1], axis[3])[j]
+
+    def ocopy(col, f, s, part, sem, to_f, to_s):
+        off, num = (0, ON[col]) if part is None else part
+        row = (s * 4 + f) * ON[col] + off
+        ref = (oa, ob)[col].at[pl.ds(pl.multiple_of(row, 16), num), :]
+        to = dev(to_s * 4 + to_f if col == 0 else to_f * 4 + to_s)
         return remote(ref, ref, osend.at[col], orecv.at[col, sem], to)
 
-    WAY = (1, -1)
-
-    @step
     def _o0(col, i):
         need(2, loads2)
-        ocopy(col, 0, 0, 0, i, WAY[i], 0).start()
-
-    @step
+        f, s = HERE[col]
+        ocopy(col, f, s, None, i, AXES[col][0][0][i], s).start()
+
     def _o1(col, i):
-        ocopy(col, -WAY[i], 0, 0, i, WAY[i], 0).wait_recv()
-        ocopy(col, -WAY[i], 0, 1 + i, 2 + i, WAY[i], 0).start()
-
-    @step
+        send, recv, way, _, parts = AXES[col][0]
+        s, w = HERE[col][1], way[i]
+        ocopy(col, recv[i], s, None, i, send[i], s).wait_recv()
+        if parts[col][w][1]:
+            ocopy(col, recv[i], s, parts[col][w], 2 + w, send[w], s).start()
+
     def _o3(col):
-        ocopy(col, 2, 0, 1, 2, 1, 0).wait_recv()
-        ocopy(col, 2, 0, 2, 3, 1, 0).wait_recv()
-
-    @step
+        send, _, _, far, parts = AXES[col][0]
+        s = HERE[col][1]
+        for w in range(2):
+            if parts[col][w][1]:
+                ocopy(col, far, s, parts[col][w], 2 + w, send[w], s).wait_recv()
+
     def _os(col, j, i):
         need(2, loads2)
-        ocopy(col, JF[j], 0, 0, 4 + 2 * j + i, 0, WAY[i]).start()
-
-    @step
+        f, s = HERE[col]
+        ocopy(col, first_of(col, j), s, None, 4 + 2 * j + i, f, AXES[col][1][0][i]).start()
+
     def _of(col, j, i):
-        ocopy(col, JF[j], -WAY[i], 0, 4 + 2 * j + i, 0, WAY[i]).wait_recv()
-        ocopy(col, JF[j], -WAY[i], 1 + i, 12 + 2 * j + i, 0, WAY[i]).start()
+        send, recv, way, _, parts = AXES[col][1]
+        f, w = HERE[col][0], way[i]
+        fj = first_of(col, j)
+        ocopy(col, fj, recv[i], None, 4 + 2 * j + i, f, send[i]).wait_recv()
+        if parts[col][w][1]:
+            ocopy(col, fj, recv[i], parts[col][w], 12 + 2 * j + w, f, send[w]).start()
+
+    def ofar(col):
+        send, _, _, far, parts = AXES[col][1]
+        f = HERE[col][0]
+        for j in range(4):
+            for w in range(2):
+                if parts[col][w][1]:
+                    ocopy(
+                        col, first_of(col, j), far, parts[col][w], 12 + 2 * j + w, f, send[w]
+                    ).wait_recv()
 
     CC = (b, nb)
 
@@ -291,69 +293,50 @@
     to_y = (to_yp, to_ym)
 
     def xsem(cc, k):
-        return cc * 11 + k
-
-    @step
-    def _pn():
-        need("x", loadx)
-
-        def prenorm(i, carry):
-            rows = pl.ds(pl.multiple_of(i * 16, 16), 16)
-            h = hid[rows, :].astype(F32)
-            r = lax.rsqrt(jnp.mean(h * h, axis=-1, keepdims=True) + EPSILON)
-            to = pl.ds(pl.multiple_of(b * TOK + t * SUB + i * 16, 16), 16)
-            xs[to, :] = (h * r * pre[...]).astype(BF)
-            return carry
-
-        lax.fori_loop(0, SUB // 16, prenorm, 0)
-
-    @step
+        return cc * 12 + k
+
     def _xp(h):
-        xcopy(0, y, core, 1 + h, 22 + h, to_xq).start()
+        xcopy(0, y, core, 1 + h, 24 + h, to_xq).start()
 
     def xout(cc, h):
         for i in range(2):
             xcopy(cc, y, core, 1 + h, xsem(cc, 2 * i + h), to_y[i]).start()
         xcopy(cc, y, core, 1 + h, xsem(cc, 6 + h), to_pt).start()
 
-    @step
     def _xo(h):
         xout(0, h)
 
-    @step
     def _xg(h):
-        xcopy(1, y, core, 1 + h, 22 + h, to_xq).wait_recv()
+        xcopy(1, y, core, 1 + h, 24 + h, to_xq).wait_recv()
         xout(1, h)
 
     YB = (ym, yp)
 
-    @step
     def _xf(cc, i):
         xcopy(cc, YB[i], core, 1 + i, xsem(cc, 3 * i), to_y[i]).wait_recv()
         xcopy(cc, YB[i], core, 1 + i, xsem(cc, 4 + i), to_y[i]).start()
 
-    @step
     def _xm(cc, i):
         xcopy(cc, YB[i], core, 2 - i, xsem(cc, 1 + i), to_y[i]).wait_recv()
         xcopy(cc, YB[i], core, 0, xsem(cc, 8 + i), to_pt).start()
 
-    @step
-    def _xopp(cc):
-        xcopy(cc, yo, core, 1, xsem(cc, 4), to_yp).wait_recv()
-        xcopy(cc, yo, core, 2, xsem(cc, 5), to_ym).wait_recv()
-        xcopy(cc, yo, core, 0, xsem(cc, 10), to_pt).start()
-
-    @step
-    def _xd(cc):
-        xcopy(cc, y, other, 1, xsem(cc, 6), to_pt).wait_recv()
-        xcopy(cc, y, other, 2, xsem(cc, 7), to_pt).wait_recv()
-        xcopy(cc, ym, other, 0, xsem(cc, 8), to_pt).wait_recv()
-        xcopy(cc, yp, other, 0, xsem(cc, 9), to_pt).wait_recv()
-        xcopy(cc, yo, other, 0, xsem(cc, 10), to_pt).wait_recv()
+    def _xt(cc, i):
+        xcopy(cc, yo, core, 1 + i, xsem(cc, 4 + i), to_y[i]).wait_recv()
+        xcopy(cc, yo, core, 1 + i, xsem(cc, 10 + i), to_pt).start()
+
+    def _xd(g):
+        cc = (0, 1, 1)[g]
+        if g < 2:
+            xcopy(cc, y, other, 1, xsem(cc, 6), to_pt).wait_recv()
+            xcopy(cc, y, other, 2, xsem(cc, 7), to_pt).wait_recv()
+            xcopy(cc, ym, other, 0, xsem(cc, 8), to_pt).wait_recv()
+            xcopy(cc, yp, other, 0, xsem(cc, 9), to_pt).wait_recv()
+        if g != 1:
+            xcopy(cc, yo, other, 1, xsem(cc, 10), to_pt).wait_recv()
+            xcopy(cc, yo, other, 2, xsem(cc, 11), to_pt).wait_recv()
 
     base = WINDOW + (c - b) * TOK
 
-    @step
     def _ang():
         def angle(i, carry):
             rows = pl.ds(pl.multiple_of(i * 128, 128), 128)
@@ -367,76 +350,113 @@
 
         lax.fori_loop(0, PAIR // 128, angle, 0)
 
-    def mm(w, cc):
+    BLOCKS = (None, (y, ym, yp), (yo,))
+
+    def tokens(g, i):
+        return CC[0] * TOK + i * 128 if g == 0 else CC[1] * TOK + BLOCKS[g][i] * 128
+
+    def at(start):
+        return pl.ds(pl.multiple_of(start, 128), 128)
+
+    def mm(w, g, out, k0, kt, steps, fresh):
+        num = (TOK, 384, 128)[g]
+
         def part(i, carry):
-            ks = pl.ds(pl.multiple_of(i * KT, 128), KT)
-            rows = pl.ds(pl.multiple_of(CC[cc] * TOK, TOK), TOK)
-            acc[...] += jnp.dot(xs[rows, ks], w[ks, :], preferred_element_type=F32)
+            ks = pl.ds(pl.multiple_of(k0 + i * kt, 128), kt)
+            if g == 0:
+                rows = xs[pl.ds(pl.multiple_of(CC[0] * TOK, TOK), TOK), ks]
+            else:
+                rows = [xs[at(tokens(g, k)), ks] for k in range(num // 128)]
+                rows = jnp.concatenate(rows, axis=0) if num > 128 else rows[0]
+            out[...] += jnp.dot(rows, w[ks, :], preferred_element_type=F32)
             return carry
 
-        acc[...] = jnp.zeros((TOK, 256), F32)
-        lax.fori_loop(0, D // KT, part, 0)
-
-    def headed(i, cc, c0, gain):
-        raw = acc[pl.ds(pl.multiple_of(i * 128, 128), 128), c0:c0 + HD]
-        at = pl.ds(pl.multiple_of(CC[cc] * TOK + i * 128, 128), 128)
+        if fresh:
+            out[...] = jnp.zeros((num, 256), F32)
+        lax.fori_loop(0, steps, part, 0)
+
+    def each(g, fn):
+        if g == 0:
+
+            def go(i, carry):
+                fn(pl.multiple_of(i * 128, 128), tokens(0, i))
+                return carry
+
+            lax.fori_loop(0, 4, go, 0)
+        else:
+            for i in range((0, 3, 1)[g]):
+                fn(i * 128, tokens(g, i))
+
+    def headed(raw, tok, gain):
         r = lax.rsqrt(jnp.mean(raw * raw, axis=-1, keepdims=True) + EPSILON)
         n = raw * r * gain[...]
-        return n * cos[at, :] + pltpu.roll(n, HD // 2, 1) * sin[at, :]
-
-    def kcopy(cc, i):
-        rows = pl.ds(pl.multiple_of(WINDOW + CC[cc] * TOK, TOK), TOK)
+        return n * cos[at(tok), :] + pltpu.roll(n, HD // 2, 1) * sin[at(tok), :]
+
+    def krows(m, cc):
+        if m == 0:
+            return 0, CC[cc] * TOK, TOK
+        blk = (y, ym, yp, yo)[m - 1]
+        return blk * 128, CC[1 - cc] * TOK + blk * 128, 128
+
+    def kcopy(m, i):
+        slot, row, num = krows(m, 0)
         return remote(
-            kv.at[i, rows, :], kr.at[cc, i], krsend.at[cc, i], krrecv.at[cc, i],
-            (to_xq, to_xn)[i],
+            kv.at[i, pl.ds(pl.multiple_of(WINDOW + row, 128), num), :],
+            kr.at[0 if m == 0 else 1, i, pl.ds(pl.multiple_of(slot, 128), num), :],
+            krsend.at[i, m], krrecv.at[i, m], (to_xq, to_xn)[i],
         )
 
-    def kfinal(cc, i, half, to):
-        rows = pl.ds(pl.multiple_of(half * TOK, TOK), TOK)
+    def kfinal(m, i, cc, to):
+        slot, row, num = krows(m, cc)
         return remote(
-            kr.at[cc, i], kv.at[i, rows, :], kfsend.at[cc, i], kfrecv.at[cc, i], to
+            kr.at[0 if m == 0 else 1, i, pl.ds(pl.multiple_of(slot, 128), num), :],
+            kv.at[i, pl.ds(pl.multiple_of(row, 128), num), :],
+            kfsend.at[i, m], kfrecv.at[i, m], to,
         )
 
-    @step
-    def _mk(cc):
-        mm(w0, cc)
-
-        def keys(i, carry):
-            rows = pl.ds(pl.multiple_of(i * 128, 128), 128)
-            to = pl.ds(pl.multiple_of(WINDOW + CC[cc] * TOK + i * 128, 128), 128)
-            kv[0, to, :] = headed(i, cc, 0, kg_v).astype(BF)
-            kv[1, to, :] = acc[rows, HD:2 * HD].astype(BF)
-            return carry
-
-        lax.fori_loop(0, 4, keys, 0)
+    def _mk(g):
+        mm(w0, g, acc.at[pl.ds(0, (TOK, 384, 128)[g]), :], 0, KT, D // KT, True)
+
+        def keys(row, tok):
+            raw = acc[pl.ds(row, 128), 0:HD]
+            kv[0, at(WINDOW + tok), :] = headed(raw, tok, kg_v).astype(BF)
+            kv[1, at(WINDOW + tok), :] = acc[pl.ds(row, 128), HD:2 * HD].astype(BF)
+
+        each(g, keys)
 
         @pl.when(c < 14)
         def _():
-            kcopy(cc, 0).start()
-            kcopy(cc, 1).start()
-
-    @step
-    def _kvf(cc, i):
+            for m in ((0,), (1, 2, 3), (4,))[g]:
+                for i in range(2):
+                    kcopy(m, i).start()
+
+    def _kvf(m, i):
         src = (cq, cn)[i]
 
         @pl.when(src < 14)
         def _():
-            kcopy(cc, i).wait_recv()
-            kfinal(cc, i, CC[1 - cc], dev((src + 2) % 16)).start()
-
-    @step
-    def _mq(cc):
-        mm(w1, cc)
-
-        def queries(i, carry):
-            to = pl.ds(pl.multiple_of(CC[cc] * TOK + i * 128, 128), 128)
+            kcopy(m, i).wait_recv()
+            kfinal(m, i, 1, dev((src + 2) % 16)).start()
+
+    def qhalf(g, second):
+        start = (0, TOK, TOK + 384)[g]
+        out = accq.at[pl.ds(start, (TOK, 384, 128)[g]), :]
+        z2 = 1 - z // 2 if second else z // 2
+        mm(w1, g, out, z2 * (D // 2), QT, D // 2 // QT, not second)
+
+    def _mqa(g):
+        qhalf(g, False)
+
+    def _mqb(g):
+        qhalf(g, True)
+
+        def queries(row, tok):
             for h in range(2):
-                qb[h, to, :] = (headed(i, cc, h * HD, qg_v) * QUERY_FACTOR).astype(BF)
-            return carry
-
-        lax.fori_loop(0, 4, queries, 0)
-
-    @step
+                raw = accq[pl.ds((0, TOK, TOK + 384)[g] + row, 128), h * HD:(h + 1) * HD]
+                qb[h, at(tok), :] = (headed(raw, tok, qg_v) * QUERY_FACTOR).astype(BF)
+
+        each(g, queries)
+
     def _aw():
         @pl.when(c < 2)
         def _():
@@ -445,9 +465,9 @@
 
         @pl.when(c >= 2)
         def _():
-            for cc in range(2):
+            for m in range(5):
                 for i in range(2):
-                    kfinal(cc, i, CC[cc], to_xq).wait_recv()
+                    kfinal(m, i, 0, to_xq).wait_recv()
 
     first = WINDOW - start_s[0] - (c - b) * TOK
 
@@ -470,20 +490,17 @@
         half = nb if from_pair else b
         return remote(ast.at[rows, :], att.at[half, rows, :], swsend.at[i], swrecv.at[i], to_xq)
 
-    @step
     def _au(i):
         o = attend(pl.multiple_of(nb * TOK + i * 128, 128))
         ast[i * 128:(i + 1) * 128, 0:128] = o[:128]
         ast[i * 128:(i + 1) * 128, 128:256] = o[128:]
         swap(i, False).start()
 
-    @step
     def _ao(i):
         o = attend(pl.multiple_of(b * TOK + i * 128, 128))
         att[b, i * 128:(i + 1) * 128, 0:128] = o[:128]
         att[b, i * 128:(i + 1) * 128, 128:256] = o[128:]
 
-    @step
     def _sw():
         for i in range(4):
             swap(i, True).wait_recv()
@@ -492,7 +509,8 @@
 
     def at_s(q):
         col, j = CHUNKS[q]
-        return nxt(fs(col)[1], JF[j])
+        axis = AXES[col][1]
+        return (HERE[col][1], axis[1][0], axis[1][1], axis[3])[j]
 
     def wide(q):
         return pl.ds(0, CWP[CHUNKS[q][0]])
@@ -518,13 +536,10 @@
         w = CWP[CHUNKS[q][0]]
         return pp[q, yy, core, :, 0:w].astype(F32) + dd[q, yy, :, 0:w].astype(F32)
 
-    @step
     def _pj(q):
         col, j = CHUNKS[q]
         if j == 3:
-            for k in range(4):
-                for i in range(2):
-                    ocopy(col, JF[k], 2, 1 + i, 12 + 2 * k + i, 0, 1).wait_recv()
+            ofar(col)
         n = CW[col]
         wref = (oa, ob)[col]
         rows = pl.ds(pl.multiple_of(at_s(q) * n, 16), n)
@@ -546,7 +561,6 @@
         lax.fori_loop(0, 2, part, 0)
         r0copy(q).start()
 
-    @step
     def _r1(q):
         w = CWP[CHUNKS[q][0]]
         r0copy(q).wait_recv()
@@ -554,7 +568,6 @@
         r1copy(q, 0).start()
         r1copy(q, 1).start()
 
-    @step
     def _r2(q, i):
         w = CWP[CHUNKS[q][0]]
         r1copy(q, i).wait_recv()
@@ -565,7 +578,6 @@
         cb[q, 1 + i, rest, 0:w] = a[rest].astype(BF)
         r2copy(q, i).start()
 
-    @step
     def _r3(q):
         w = CWP[CHUNKS[q][0]]
         r2copy(q, 0).wait_recv()
@@ -573,16 +585,42 @@
         v = both(q, y) + gg[q, 0, :, 0:w].astype(F32) + gg[q, 1, :, 0:w].astype(F32)
         (sa, sb)[CHUNKS[q][0]][at_s(q)] = v
 
-    @step
     def _zero():
         for q in range(8):
-            if CHUNKS[q][0] == 0:
+            if CHUNKS[q][0] == 1:
                 for g in range(8):
                     pp[q, g // 2, g % 2, :, 512:640] = jnp.zeros((SUB, 128), BF)
 
-    for line in ORDER:
-        name, *nums = line.split(",")
-        steps[name](*[int(v) for v in nums])
+    for fn, *nums in (
+        (_xo, 1), (_ww, 0), (_xp, 1), (_wz0, 1), (_o0, 1, 1), (_o0, 1, 0), (_xo, 0),
+        (_wfw, 1, 0, 1), (_o0, 0, 1), (_wz0, 0), (_wzx, 0, 1), (_wzx, 0, 2), (_xp, 0),
+        (_wr, 0), (_o1, 0, 1), (_wf, 0, 1), (_xg, 1), (_wfw, 1, 0, 0), (_o1, 1, 1),
+        (_o1, 1, 0), (_o0, 0, 0), (_ww, 1), (_wzx, 1, 2), (_wr, 1), (_xg, 0), (_xf, 0, 0),
+        (_wf, 0, 0), (_wfw, 0, 2, 1), (_os, 1, 1, 1), (_wfw, 0, 0, 0), (_wf, 1, 1), (_wzo, 0),
+        (_xf, 0, 1), (_os, 1, 0, 0), (_wfw, 0, 0, 1), (_wfw, 0, 1, 0), (_os, 1, 2, 1),
+        (_xf, 1, 1), (_os, 1, 2, 0), (_o1, 0, 0), (_wfw, 0, 1, 1), (_xm, 0, 0),
+        (_of, 1, 1, 1), (_ang,), (_zero,), (_wfw, 0, 2, 0), (_o3, 1), (_wfw, 0, 3, 1),
+        (_xm, 1, 1), (_wf, 1, 0), (_xf, 1, 0), (_xm, 0, 1), (_wfw, 0, 3, 0), (_xm, 1, 0),
+        (_wzx, 1, 1), (_os, 1, 3, 1), (_wzo, 1), (_xd, 1), (_wl, 0), (_wfw, 1, 2, 1),
+        (_xt, 0, 1), (_xt, 0, 0), (_mk, 1), (_wfw, 1, 1, 1), (_xd, 0), (_mk, 0),
+        (_wfw, 1, 2, 0), (_kvf, 3, 1), (_xt, 1, 0), (_wfw, 1, 3, 0), (_of, 1, 2, 1),
+        (_wfw, 1, 3, 1), (_kvf, 1, 0), (_kvf, 3, 0), (_kvf, 2, 1), (_kvf, 2, 0),
+        (_wfw, 1, 1, 0), (_os, 0, 0, 0), (_kvf, 1, 1), (_xt, 1, 1), (_os, 0, 2, 1), (_xd, 2),
+        (_mk, 2), (_kvf, 0, 1), (_kvf, 0, 0), (_o3, 0), (_mqa, 0), (_mqa, 1), (_os, 0, 3, 0),
+        (_mqa, 2), (_os, 0, 3, 1), (_os, 0, 0, 1), (_kvf, 4, 1), (_kvf, 4, 0), (_wl, 1),
+        (_mqb, 1), (_of, 1, 3, 1), (_mqb, 2), (_os, 0, 1, 0), (_os, 0, 1, 1), (_of, 0, 2, 1),
+        (_os, 0, 2, 0), (_os, 1, 0, 1), (_aw,), (_au, 0), (_au, 1), (_au, 2), (_au, 3),
+        (_os, 1, 3, 0), (_mqb, 0), (_ao, 0), (_ao, 1), (_ao, 2), (_ao, 3), (_sw,), (_pj, 1),
+        (_os, 1, 1, 0), (_of, 0, 3, 0), (_of, 1, 2, 0), (_of, 1, 0, 1), (_pj, 0), (_r1, 1),
+        (_pj, 5), (_r1, 0), (_of, 1, 3, 0), (_of, 0, 1, 0), (_r1, 5), (_of, 1, 0, 0),
+        (_r2, 1, 1), (_r2, 1, 0), (_of, 0, 1, 1), (_of, 0, 0, 0), (_r2, 0, 0), (_r2, 0, 1),
+        (_of, 0, 2, 0), (_of, 0, 3, 1), (_pj, 2), (_of, 1, 1, 0), (_pj, 4), (_r1, 2),
+        (_r2, 5, 0), (_of, 0, 0, 1), (_r1, 4), (_pj, 3), (_r2, 5, 1), (_r1, 3), (_r2, 2, 0),
+        (_r2, 2, 1), (_r2, 4, 1), (_r3, 0), (_pj, 7), (_r2, 4, 0), (_pj, 6), (_r1, 7),
+        (_r1, 6), (_r2, 3, 0), (_r3, 1), (_r2, 3, 1), (_r3, 2), (_r3, 4), (_r2, 7, 1),
+        (_r2, 7, 0), (_r2, 6, 1), (_r3, 5), (_r2, 6, 0), (_r3, 3), (_r3, 7), (_r3, 6),
+    ):
+        fn(*nums)
 
     for i in range(16):
         zi, xi = i // 4, i % 4
@@ -605,18 +643,16 @@
         remote(ref, ref, osend.at[col], orecv.at[col, 0], to_pt).wait_send()
     ref = xs.at[pl.ds(0, 15 * SUB), :]
     remote(ref, ref, xsend, xrecv.at[0], to_pt).wait_send()
-    for half in range(2):
-
-        @pl.when(c < 14)
-        def _():
-            for i in range(2):
-                kcopy(half, i).wait_send()
-
+    for m in range(5):
         for i in range(2):
+
+            @pl.when(c < 14)
+            def _():
+                kcopy(m, i).wait_send()
 
             @pl.when((cq, cn)[i] < 14)
             def _():
-                kfinal(half, i, b, to_xq).wait_send()
+                kfinal(m, i, 1, to_xq).wait_send()
 
     for i in range(4):
         swap(i, False).wait_send()
@@ -650,7 +686,7 @@
             pltpu.VMEM((2, WINDOW + PAIR, HD), BF), pltpu.VMEM((2, 2, TOK, HD), BF),
             pltpu.VMEM((2, PAIR, HD), BF),
             pltpu.VMEM((2, TOK, 256), BF), pltpu.VMEM((TOK, 256), BF),
-            pltpu.VMEM((TOK, 256), F32),
+            pltpu.VMEM((TOK, 256), F32), pltpu.VMEM((PAIR, 256), F32),
             pltpu.VMEM((SUB, D), BF), pltpu.VMEM((1, D), F32), pltpu.VMEM((1, D), F32),
             pltpu.VMEM((PAIR, HD), F32), pltpu.VMEM((PAIR, HD), F32),
             pltpu.VMEM((8, 4, 2, SUB, 768), BF),
@@ -660,8 +696,8 @@
             pltpu.VMEM((8, 3, SUB, 768), BF),
             pltpu.VMEM((4, SUB, CWP[0]), F32), pltpu.VMEM((4, SUB, CWP[1]), F32),
             pltpu.VMEM((SUB, D), F32),
-            dma((16,)), dma((2,)), dma((2, 22)), dma((2,)), dma((2, 20)), dma, dma((24,)),
-            dma((2, 2)), dma((2, 2)), dma((2, 2)), dma((2, 2)), dma((4,)), dma((4,)),
+            dma((16,)), dma((2,)), dma((2, 22)), dma((2,)), dma((2, 20)), dma, dma((26,)),
+            dma((2, 5)), dma((2, 5)), dma((2, 5)), dma((2, 5)), dma((4,)), dma((4,)),
             dma((8, 5)), dma((8, 5)),
         ],
         compiler_params=pltpu.CompilerParams(

time: 126 us -> 120 us (0.952)
  Pallas kernels: 123 us -> 117 us
    pallas_call x1, Pallas kernels: 123 us -> 117 us  [local(): pl.pallas_call(body, out_shape=jax.ShapeDtypeStruct((SUB, D), BF), in_spe...]
where the time goes in v4:
time: 120 us
  Pallas kernels  117 us (98%)
  local copies, waits for them, and re-layouts  1.99 us (2%)
    pallas_call x1, Pallas kernels, local(): pl.pallas_call(body, out_shape=jax.ShapeDtypeStruct((SUB, D), BF), in_spe...  117 us

profile of v4, /device:TPU:32, one launch (start us, length us, event | category | flops | bytes accessed | tf_op | source)
XLA Modules:
  0.0 120.1 jit_solution(4138708073770964109)
XLA Ops:
  0.7 0.6 maximum_bitcast_fusion.freq_v
  1.3 116.9 %layer.1 = bf16[64,5376]{1,0:T(8,128)(2,1)} custom-call(bf16[64,5376]{1,0:T(8,128)(2,1)} %hid_h.1, s32[1]{0:T(128)S(6)} %copy.14.start_s, f32[5376]{0:T(1024)} %pre_h.1, bf16[336,512]{1,0:T(8,128)(2,1)} %q_h.1, bf16[336,256]{1,0:T(8,128)(2,1)} %k_h.1, bf16[336,256]{1,0:T(8,128)(2,1)} %v_h.1, bf16[336,512]{1,0:T(8,128)(2,1)} %bitcast.5, f32[1,128]{1,0:T(1,128)} %bitcast.6, ...), custom_call_target="tpu_custom_call" | custom-call | tf_op jit(solution)/shard_map/layer/pallas_call | solution.py:676
  118.1 2.0 %copy.15 = bf16[64,5376]{1,0:T(8,128)(2,1)} copy(bf16[64,5376]{1,0:T(8,128)(2,1)} %layer.1) | data formatting | bytes 1376256
  (1 shorter events, 0.0 us)

commit v5 on v4

--- a/solution.py
+++ b/solution.py
@@ -22,8 +22,7 @@
 OZ = ((0, 96), (96, 96)), ((0, 80), (80, 64))
 CW = (768, 576)
 CWP = (768, 640)
-KT = 2688
-QT = 2688
+KT = 768
 BF = jnp.bfloat16
 F32 = jnp.float32
 
@@ -31,7 +30,7 @@
 def body(
     hid_h, start_s, pre_h, q_h, k_h, v_h, o_h, qg_v, kg_v, pk_h, pv_h, post_h, freq_v,
     out_v,
-    w0, w1, oa, ob, ow, rb, xs, kv, kr, qb, att, ast, acc, accq, hid, pre, post, cos, sin,
+    w0, w1, oa, ob, ow, rb, xs, kv, kr, qb, att, ast, acc, hid, pre, post, cos, sin,
     pp, dd, ee, gg, cb, sa, sb, full,
     lsem, wsend, wrecv, osend, orecv, xsend, xrecv, krsend, krrecv, kfsend, kfrecv,
     swsend, swrecv, rsend, rrecv,
@@ -140,6 +139,9 @@
         return carry
 
     lax.fori_loop(0, SUB // 16, prenorm, 0)
+    for q in (1, 4, 5, 7):
+        for g in range(8):
+            pp[q, g // 2, g % 2, :, 512:640] = jnp.zeros((SUB, 128), BF)
     pl.semaphore_wait(barrier, len(peers))
 
     waited = set()
@@ -358,22 +360,21 @@
     def at(start):
         return pl.ds(pl.multiple_of(start, 128), 128)
 
-    def mm(w, g, out, k0, kt, steps, fresh):
+    def mm(w, g):
         num = (TOK, 384, 128)[g]
 
         def part(i, carry):
-            ks = pl.ds(pl.multiple_of(k0 + i * kt, 128), kt)
+            ks = pl.ds(pl.multiple_of(i * KT, 128), KT)
             if g == 0:
                 rows = xs[pl.ds(pl.multiple_of(CC[0] * TOK, TOK), TOK), ks]
             else:
                 rows = [xs[at(tokens(g, k)), ks] for k in range(num // 128)]
                 rows = jnp.concatenate(rows, axis=0) if num > 128 else rows[0]
-            out[...] += jnp.dot(rows, w[ks, :], preferred_element_type=F32)
+            acc[0:num] += jnp.dot(rows, w[ks, :], preferred_element_type=F32)
             return carry
 
-        if fresh:
-            out[...] = jnp.zeros((num, 256), F32)
-        lax.fori_loop(0, steps, part, 0)
+        acc[0:num] = jnp.zeros((num, 256), F32)
+        lax.fori_loop(0, D // KT, part, 0)
 
     def each(g, fn):
         if g == 0:
@@ -387,7 +388,8 @@
             for i in range((0, 3, 1)[g]):
                 fn(i * 128, tokens(g, i))
 
-    def headed(raw, tok, gain):
+    def headed(row, tok, c0, gain):
+        raw = acc[pl.ds(row, 128), c0:c0 + HD]
         r = lax.rsqrt(jnp.mean(raw * raw, axis=-1, keepdims=True) + EPSILON)
         n = raw * r * gain[...]
         return n * cos[at(tok), :] + pltpu.roll(n, HD // 2, 1) * sin[at(tok), :]
@@ -415,11 +417,10 @@
         )
 
     def _mk(g):
-        mm(w0, g, acc.at[pl.ds(0, (TOK, 384, 128)[g]), :], 0, KT, D // KT, True)
+        mm(w0, g)
 
         def keys(row, tok):
-            raw = acc[pl.ds(row, 128), 0:HD]
-            kv[0, at(WINDOW + tok), :] = headed(raw, tok, kg_v).astype(BF)
+            kv[0, at(WINDOW + tok), :] = headed(row, tok, 0, kg_v).astype(BF)
             kv[1, at(WINDOW + tok), :] = acc[pl.ds(row, 128), HD:2 * HD].astype(BF)
 
         each(g, keys)
@@ -438,22 +439,13 @@
             kcopy(m, i).wait_recv()
             kfinal(m, i, 1, dev((src + 2) % 16)).start()
 
-    def qhalf(g, second):
-        start = (0, TOK, TOK + 384)[g]
-        out = accq.at[pl.ds(start, (TOK, 384, 128)[g]), :]
-        z2 = 1 - z // 2 if second else z // 2
-        mm(w1, g, out, z2 * (D // 2), QT, D // 2 // QT, not second)
-
-    def _mqa(g):
-        qhalf(g, False)
-
-    def _mqb(g):
-        qhalf(g, True)
+    def _mq(g):
+        mm(w1, g)
 
         def queries(row, tok):
             for h in range(2):
-                raw = accq[pl.ds((0, TOK, TOK + 384)[g] + row, 128), h * HD:(h + 1) * HD]
-                qb[h, at(tok), :] = (headed(raw, tok, qg_v) * QUERY_FACTOR).astype(BF)
+                q = headed(row, tok, h * HD, qg_v) * QUERY_FACTOR
+                qb[h, at(tok), :] = q.astype(BF)
 
         each(g, queries)
 
@@ -585,40 +577,34 @@
         v = both(q, y) + gg[q, 0, :, 0:w].astype(F32) + gg[q, 1, :, 0:w].astype(F32)
         (sa, sb)[CHUNKS[q][0]][at_s(q)] = v
 
-    def _zero():
-        for q in range(8):
-            if CHUNKS[q][0] == 1:
-                for g in range(8):
-                    pp[q, g // 2, g % 2, :, 512:640] = jnp.zeros((SUB, 128), BF)
-
     for fn, *nums in (
-        (_xo, 1), (_ww, 0), (_xp, 1), (_wz0, 1), (_o0, 1, 1), (_o0, 1, 0), (_xo, 0),
-        (_wfw, 1, 0, 1), (_o0, 0, 1), (_wz0, 0), (_wzx, 0, 1), (_wzx, 0, 2), (_xp, 0),
-        (_wr, 0), (_o1, 0, 1), (_wf, 0, 1), (_xg, 1), (_wfw, 1, 0, 0), (_o1, 1, 1),
-        (_o1, 1, 0), (_o0, 0, 0), (_ww, 1), (_wzx, 1, 2), (_wr, 1), (_xg, 0), (_xf, 0, 0),
-        (_wf, 0, 0), (_wfw, 0, 2, 1), (_os, 1, 1, 1), (_wfw, 0, 0, 0), (_wf, 1, 1), (_wzo, 0),
-        (_xf, 0, 1), (_os, 1, 0, 0), (_wfw, 0, 0, 1), (_wfw, 0, 1, 0), (_os, 1, 2, 1),
-        (_xf, 1, 1), (_os, 1, 2, 0), (_o1, 0, 0), (_wfw, 0, 1, 1), (_xm, 0, 0),
-        (_of, 1, 1, 1), (_ang,), (_zero,), (_wfw, 0, 2, 0), (_o3, 1), (_wfw, 0, 3, 1),
-        (_xm, 1, 1), (_wf, 1, 0), (_xf, 1, 0), (_xm, 0, 1), (_wfw, 0, 3, 0), (_xm, 1, 0),
-        (_wzx, 1, 1), (_os, 1, 3, 1), (_wzo, 1), (_xd, 1), (_wl, 0), (_wfw, 1, 2, 1),
-        (_xt, 0, 1), (_xt, 0, 0), (_mk, 1), (_wfw, 1, 1, 1), (_xd, 0), (_mk, 0),
-        (_wfw, 1, 2, 0), (_kvf, 3, 1), (_xt, 1, 0), (_wfw, 1, 3, 0), (_of, 1, 2, 1),
-        (_wfw, 1, 3, 1), (_kvf, 1, 0), (_kvf, 3, 0), (_kvf, 2, 1), (_kvf, 2, 0),
-        (_wfw, 1, 1, 0), (_os, 0, 0, 0), (_kvf, 1, 1), (_xt, 1, 1), (_os, 0, 2, 1), (_xd, 2),
-        (_mk, 2), (_kvf, 0, 1), (_kvf, 0, 0), (_o3, 0), (_mqa, 0), (_mqa, 1), (_os, 0, 3, 0),
-        (_mqa, 2), (_os, 0, 3, 1), (_os, 0, 0, 1), (_kvf, 4, 1), (_kvf, 4, 0), (_wl, 1),
-        (_mqb, 1), (_of, 1, 3, 1), (_mqb, 2), (_os, 0, 1, 0), (_os, 0, 1, 1), (_of, 0, 2, 1),
-        (_os, 0, 2, 0), (_os, 1, 0, 1), (_aw,), (_au, 0), (_au, 1), (_au, 2), (_au, 3),
-        (_os, 1, 3, 0), (_mqb, 0), (_ao, 0), (_ao, 1), (_ao, 2), (_ao, 3), (_sw,), (_pj, 1),
-        (_os, 1, 1, 0), (_of, 0, 3, 0), (_of, 1, 2, 0), (_of, 1, 0, 1), (_pj, 0), (_r1, 1),
-        (_pj, 5), (_r1, 0), (_of, 1, 3, 0), (_of, 0, 1, 0), (_r1, 5), (_of, 1, 0, 0),
-        (_r2, 1, 1), (_r2, 1, 0), (_of, 0, 1, 1), (_of, 0, 0, 0), (_r2, 0, 0), (_r2, 0, 1),
-        (_of, 0, 2, 0), (_of, 0, 3, 1), (_pj, 2), (_of, 1, 1, 0), (_pj, 4), (_r1, 2),
-        (_r2, 5, 0), (_of, 0, 0, 1), (_r1, 4), (_pj, 3), (_r2, 5, 1), (_r1, 3), (_r2, 2, 0),
-        (_r2, 2, 1), (_r2, 4, 1), (_r3, 0), (_pj, 7), (_r2, 4, 0), (_pj, 6), (_r1, 7),
-        (_r1, 6), (_r2, 3, 0), (_r3, 1), (_r2, 3, 1), (_r3, 2), (_r3, 4), (_r2, 7, 1),
-        (_r2, 7, 0), (_r2, 6, 1), (_r3, 5), (_r2, 6, 0), (_r3, 3), (_r3, 7), (_r3, 6),
+        (_wz0, 1), (_o0, 1, 0), (_ww, 0), (_o0, 1, 1), (_os, 1, 0, 1), (_xp, 0), (_wr, 0),
+        (_o0, 0, 1), (_xo, 0), (_xp, 1), (_wzx, 0, 2), (_wr, 1), (_xo, 1), (_wz0, 0),
+        (_o1, 1, 1), (_o1, 1, 0), (_wzx, 0, 1), (_wf, 0, 1), (_ww, 1), (_xg, 0), (_wf, 1, 1),
+        (_wfw, 0, 0, 0), (_os, 1, 2, 1), (_wf, 0, 0), (_ang,), (_o1, 0, 1),
+        (_wfw, 0, 2, 1), (_os, 1, 1, 1), (_wfw, 0, 0, 1), (_wfw, 0, 2, 0), (_wzx, 1, 2),
+        (_xg, 1), (_xf, 0, 0), (_wf, 1, 0), (_o0, 0, 0), (_xf, 0, 1), (_xf, 1, 0), (_wzo, 0),
+        (_wzx, 1, 1), (_os, 1, 1, 0), (_wfw, 0, 1, 1), (_wfw, 0, 1, 0), (_wfw, 0, 3, 0),
+        (_wfw, 1, 2, 0), (_xm, 1, 0), (_xf, 1, 1), (_o3, 1), (_xm, 1, 1), (_os, 1, 2, 0),
+        (_wfw, 0, 3, 1), (_os, 1, 3, 1), (_os, 1, 3, 0), (_of, 1, 0, 1), (_wfw, 1, 2, 1),
+        (_xd, 1), (_xm, 0, 0), (_wzo, 1), (_wfw, 1, 0, 1), (_o1, 0, 0), (_wfw, 1, 0, 0),
+        (_wl, 0), (_xt, 0, 0), (_of, 1, 2, 1), (_xm, 0, 1), (_wfw, 1, 1, 0), (_xt, 0, 1),
+        (_mk, 1), (_xd, 0), (_wfw, 1, 1, 1), (_mk, 0), (_kvf, 2, 1), (_kvf, 2, 0),
+        (_wfw, 1, 3, 1), (_of, 1, 1, 1), (_os, 0, 0, 1), (_wfw, 1, 3, 0), (_xt, 1, 0),
+        (_xt, 1, 1), (_o3, 0), (_kvf, 3, 0), (_os, 0, 3, 0), (_kvf, 3, 1), (_xd, 2), (_mk, 2),
+        (_os, 0, 0, 0), (_os, 0, 1, 0), (_kvf, 0, 0), (_os, 0, 1, 1), (_of, 1, 3, 1),
+        (_kvf, 0, 1), (_os, 0, 3, 1), (_kvf, 1, 0), (_kvf, 1, 1), (_wl, 1), (_mq, 0),
+        (_kvf, 4, 1), (_kvf, 4, 0), (_mq, 1), (_mq, 2), (_aw,), (_au, 0), (_au, 1), (_au, 2),
+        (_os, 0, 2, 1), (_au, 3), (_of, 0, 1, 1), (_of, 1, 2, 0), (_ao, 0), (_os, 0, 2, 0),
+        (_ao, 1), (_of, 0, 0, 1), (_of, 0, 3, 0), (_os, 1, 0, 0), (_of, 0, 3, 1), (_ao, 2),
+        (_ao, 3), (_sw,), (_pj, 1), (_pj, 0), (_pj, 5), (_r1, 1), (_of, 0, 2, 1), (_pj, 3),
+        (_r1, 0), (_of, 1, 0, 0), (_r1, 5), (_of, 0, 1, 0), (_of, 1, 1, 0), (_of, 0, 0, 0),
+        (_of, 0, 2, 0), (_of, 1, 3, 0), (_r1, 3), (_r2, 1, 0), (_r2, 1, 1), (_r2, 0, 0),
+        (_pj, 4), (_r2, 5, 1), (_pj, 2), (_r1, 4), (_r2, 3, 0), (_r2, 3, 1), (_r1, 2),
+        (_pj, 6), (_r2, 4, 0), (_r2, 0, 1), (_r3, 1), (_r1, 6), (_r2, 4, 1), (_r2, 5, 0),
+        (_pj, 7), (_r1, 7), (_r2, 2, 1), (_r3, 0), (_r3, 3), (_r2, 6, 0), (_r2, 2, 0),
+        (_r2, 6, 1), (_r2, 7, 1), (_r2, 7, 0), (_r3, 2), (_r3, 6), (_r3, 5), (_r3, 4),
+        (_r3, 7),
     ):
         fn(*nums)
 
@@ -686,7 +672,7 @@
             pltpu.VMEM((2, WINDOW + PAIR, HD), BF), pltpu.VMEM((2, 2, TOK, HD), BF),
             pltpu.VMEM((2, PAIR, HD), BF),
             pltpu.VMEM((2, TOK, 256), BF), pltpu.VMEM((TOK, 256), BF),
-            pltpu.VMEM((TOK, 256), F32), pltpu.VMEM((PAIR, 256), F32),
+            pltpu.VMEM((TOK, 256), F32),
             pltpu.VMEM((SUB, D), BF), pltpu.VMEM((1, D), F32), pltpu.VMEM((1, D), F32),
             pltpu.VMEM((PAIR, HD), F32), pltpu.VMEM((PAIR, HD), F32),
             pltpu.VMEM((8, 4, 2, SUB, 768), BF),

time: 120 us -> 118 us (0.983)
  Pallas kernels: 117 us -> 115 us
    pallas_call x1, Pallas kernels: 117 us -> 115 us  [local(): pl.pallas_call(body, out_shape=jax.ShapeDtypeStruct((SUB, D), BF), in_spe...]
where the time goes in v5:
time: 118 us
  Pallas kernels  115 us (97%)
  local copies, waits for them, and re-layouts  1.99 us (2%)
    pallas_call x1, Pallas kernels, local(): pl.pallas_call(body, out_shape=jax.ShapeDtypeStruct((SUB, D), BF), in_spe...  115 us

profile of v5, /device:TPU:32, one launch (start us, length us, event | category | flops | bytes accessed | tf_op | source)
XLA Modules:
  0.0 117.8 jit_solution(9065816002525494496)
XLA Ops:
  0.7 0.6 maximum_bitcast_fusion.freq_v
  1.3 114.5 %layer.1 = bf16[64,5376]{1,0:T(8,128)(2,1)} custom-call(bf16[64,5376]{1,0:T(8,128)(2,1)} %hid_h.1, s32[1]{0:T(128)S(6)} %copy.14.start_s, f32[5376]{0:T(1024)} %pre_h.1, bf16[336,512]{1,0:T(8,128)(2,1)} %q_h.1, bf16[336,256]{1,0:T(8,128)(2,1)} %k_h.1, bf16[336,256]{1,0:T(8,128)(2,1)} %v_h.1, bf16[336,512]{1,0:T(8,128)(2,1)} %bitcast.5, f32[1,128]{1,0:T(1,128)} %bitcast.6, ...), custom_call_target="tpu_custom_call" | custom-call | tf_op jit(solution)/shard_map/layer/pallas_call | solution.py:662
  115.8 2.0 %copy.15 = bf16[64,5376]{1,0:T(8,128)(2,1)} copy(bf16[64,5376]{1,0:T(8,128)(2,1)} %layer.1) | data formatting | bytes 1376256
  (1 shorter events, 0.0 us)

commit v6 on v5

--- a/solution.py
+++ b/solution.py
@@ -142,6 +142,20 @@
     for q in (1, 4, 5, 7):
         for g in range(8):
             pp[q, g // 2, g % 2, :, 512:640] = jnp.zeros((SUB, 128), BF)
+    base = WINDOW + (c - b) * TOK
+
+    def angle(i, carry):
+        rows = pl.ds(pl.multiple_of(i * 128, 128), 128)
+        pos = lax.broadcasted_iota(jnp.int32, (128, HD), 0) + (base + i * 128)
+        a = pos.astype(F32) * freq_v[...]
+        lane = lax.broadcasted_iota(jnp.int32, (128, HD), 1)
+        cos[rows, :] = jnp.cos(a)
+        sn = jnp.sin(a)
+        sin[rows, :] = jnp.where(lane < HD // 2, -sn, sn)
+        return carry
+
+    lax.fori_loop(0, PAIR // 128, angle, 0)
+
     pl.semaphore_wait(barrier, len(peers))
 
     waited = set()
@@ -336,21 +350,6 @@
         if g != 1:
             xcopy(cc, yo, other, 1, xsem(cc, 10), to_pt).wait_recv()
             xcopy(cc, yo, other, 2, xsem(cc, 11), to_pt).wait_recv()
-
-    base = WINDOW + (c - b) * TOK
-
-    def _ang():
-        def angle(i, carry):
-            rows = pl.ds(pl.multiple_of(i * 128, 128), 128)
-            pos = lax.broadcasted_iota(jnp.int32, (128, HD), 0) + (base + i * 128)
-            a = pos.astype(F32) * freq_v[...]
-            lane = lax.broadcasted_iota(jnp.int32, (128, HD), 1)
-            cos[rows, :] = jnp.cos(a)
-            sn = jnp.sin(a)
-            sin[rows, :] = jnp.where(lane < HD // 2, -sn, sn)
-            return carry
-
-        lax.fori_loop(0, PAIR // 128, angle, 0)
 
     BLOCKS = (None, (y, ym, yp), (yo,))
 
@@ -581,7 +580,7 @@
         (_wz0, 1), (_o0, 1, 0), (_ww, 0), (_o0, 1, 1), (_os, 1, 0, 1), (_xp, 0), (_wr, 0),
         (_o0, 0, 1), (_xo, 0), (_xp, 1), (_wzx, 0, 2), (_wr, 1), (_xo, 1), (_wz0, 0),
         (_o1, 1, 1), (_o1, 1, 0), (_wzx, 0, 1), (_wf, 0, 1), (_ww, 1), (_xg, 0), (_wf, 1, 1),
-        (_wfw, 0, 0, 0), (_os, 1, 2, 1), (_wf, 0, 0), (_ang,), (_o1, 0, 1),
+        (_wfw, 0, 0, 0), (_os, 1, 2, 1), (_wf, 0, 0), (_o1, 0, 1),
         (_wfw, 0, 2, 1), (_os, 1, 1, 1), (_wfw, 0, 0, 1), (_wfw, 0, 2, 0), (_wzx, 1, 2),
         (_xg, 1), (_xf, 0, 0), (_wf, 1, 0), (_o0, 0, 0), (_xf, 0, 1), (_xf, 1, 0), (_wzo, 0),
         (_wzx, 1, 1), (_os, 1, 1, 0), (_wfw, 0, 1, 1), (_wfw, 0, 1, 0), (_wfw, 0, 3, 0),

time: 118 us -> 119 us (level)
  no operation moved by 1% of the time
where the time goes in v6:
time: 119 us
  Pallas kernels  116 us (97%)
  local copies, waits for them, and re-layouts  1.99 us (2%)
    pallas_call x1, Pallas kernels, local(): pl.pallas_call(body, out_shape=jax.ShapeDtypeStruct((SUB, D), BF), in_spe...  116 us

profile of v6, /device:TPU:32, one launch (start us, length us, event | category | flops | bytes accessed | tf_op | source)
XLA Modules:
  0.0 118.9 jit_solution(6210498391789204088)
XLA Ops:
  0.7 0.6 maximum_bitcast_fusion.freq_v
  1.3 115.7 %layer.1 = bf16[64,5376]{1,0:T(8,128)(2,1)} custom-call(bf16[64,5376]{1,0:T(8,128)(2,1)} %hid_h.1, s32[1]{0:T(128)S(6)} %copy.14.start_s, f32[5376]{0:T(1024)} %pre_h.1, bf16[336,512]{1,0:T(8,128)(2,1)} %q_h.1, bf16[336,256]{1,0:T(8,128)(2,1)} %k_h.1, bf16[336,256]{1,0:T(8,128)(2,1)} %v_h.1, bf16[336,512]{1,0:T(8,128)(2,1)} %bitcast.5, f32[1,128]{1,0:T(1,128)} %bitcast.6, ...), custom_call_target="tpu_custom_call" | custom-call | tf_op jit(solution)/shard_map/layer/pallas_call | solution.py:661
  116.9 2.0 %copy.15 = bf16[64,5376]{1,0:T(8,128)(2,1)} copy(bf16[64,5376]{1,0:T(8,128)(2,1)} %layer.1) | data formatting | bytes 1376256
  (1 shorter events, 0.0 us)
